TPU v7x, 128 devices: a whole 4x4x4 slice. The times are simulated.
128 devices in a mesh: gx: 16 (over z, y), gy: 8 (over x, core).
Axes of the slice: x: 4, y: 4, z: 4, core: 2. Of those that a mesh axis runs over, the one named last changes fastest.
Arguments:
- fine_nodes: bfloat16 [131072, 512], P(('gx', 'gy')), may hold values from -6 to 6
- edge_latent: bfloat16 [786432, 512], P(('gx', 'gy')), may hold values from -6 to 6
- boundary: int32 [16384], P(('gx', 'gy')), may hold values from 0 to 1023, as said below
- fine_src: int32 [786432], P(('gx', 'gy')), may hold values from 0 to 2175, as said below
- fine_dst: int32 [786432], P(('gx', 'gy')), may hold values from 0 to 1023
- parent_one: int32 [131072], P(('gx', 'gy')), may hold values from 0 to 831, as said below
- weight_one: bfloat16 [131072], P(('gx', 'gy')), may hold values from 0.049804688 to 0.29882812
- coarse_src_one: int32 [196608], P(('gx', 'gy')), may hold values from 0 to 831, as said below
- coarse_dst_one: int32 [196608], P(('gx', 'gy')), may hold values from 0 to 255
- parent_two: int32 [32768], P(('gx', 'gy')), may hold values from 0 to 351, as said below
- weight_two: bfloat16 [32768], P(('gx', 'gy')), may hold values from 0.099609375 to 0.5
- coarse_src_two: int32 [49152], P(('gx', 'gy')), may hold values from 0 to 351, as said below
- coarse_dst_two: int32 [49152], P(('gx', 'gy')), may hold values from 0 to 63
- fine_message_in: bfloat16 [1536, 512], replicated, may hold values from -0.15625 to 0.15625
- fine_message_out: bfloat16 [512, 512], replicated, may hold values from -0.25 to 0.25
- fine_message_gain: bfloat16 [512], replicated, may hold values from 0.25 to 1.75
- fine_update_in: bfloat16 [1024, 512], replicated, may hold values from -0.1875 to 0.1875
- fine_update_out: bfloat16 [512, 512], replicated, may hold values from -0.25 to 0.25
- fine_update_gain: bfloat16 [512], replicated, may hold values from 0.25 to 1.75
- coarse_message_in: bfloat16 [1024, 512], replicated, may hold values from -0.1875 to 0.1875
- coarse_message_out: bfloat16 [512, 512], replicated, may hold values from -0.25 to 0.25
- coarse_message_gain: bfloat16 [512], replicated, may hold values from 0.25 to 1.75
- coarse_update_in: bfloat16 [1024, 512], replicated, may hold values from -0.1875 to 0.1875
- coarse_update_out: bfloat16 [512, 512], replicated, may hold values from -0.25 to 0.25
- coarse_update_gain: bfloat16 [512], replicated, may hold values from 0.25 to 1.75
Outputs:
- fine_out: bfloat16 [131072, 512], P(('gx', 'gy'))
Inputs may be any that keep to these rules, and one draw needn't show every extreme that they name: `boundary`: each device's 128 entries are distinct local row numbers of its own fine nodes. `fine_src`: an entry below 1024 is a local row of the edge's own device; an entry 1024 + k * 128 + r names boundary row r of the device at grid offset (k // 3 - 1, k % 3 - 1) along (gx, gy), with wrap; k is never 4. `parent_one`: an entry below 256 is a first coarse level row of the fine node's own device; an entry 256 + k * 64 + r names rim row r of the device at grid offset (k // 3 - 1, k % 3 - 1) along (gx, gy), with wrap; k is never 4. `coarse_src_one`: an entry below 256 is a first coarse level row of the edge's own device; an entry 256 + k * 64 + r names rim row r of the device at grid offset (k // 3 - 1, k % 3 - 1) along (gx, gy), with wrap; k is never 4. `parent_two`: an entry below 64 is a second coarse level row of the node's own device; an entry 64 + k * 32 + r names rim row r of the device at grid offset (k // 3 - 1, k % 3 - 1) along (gx, gy), with wrap; k is never 4. `coarse_src_two`: an entry below 64 is a second coarse level row of the edge's own device; an entry 64 + k * 32 + r names rim row r of the device at grid offset (k // 3 - 1, k % 3 - 1) along (gx, gy), with wrap; k is never 4.
All inputs are finite; a program needn't handle non-finite values.
Results may differ from a plain program's by a relative error of at most 0.012.
Values may be sent and summed in bfloat16 or wider, within the bound.
A program may use at most 128 MiB of HBM per device.

v0:
```python
import jax
import jax.numpy as jnp
from jax import lax
from jax.sharding import PartitionSpec as P

NC1_DEV = 256
NC2_DEV = 64
CB1 = 64
CB2 = 32


def padded(cells, sides, width):
    for axis, dim in sides:
        count = lax.axis_size(axis)
        head = lax.slice_in_dim(cells, 0, width, axis=dim)
        tail = lax.slice_in_dim(cells, cells.shape[dim] - width, cells.shape[dim], axis=dim)
        cells = jnp.concatenate(
            [
                lax.ppermute(tail, axis, [(i, (i + 1) % count) for i in range(count)]),
                cells,
                lax.ppermute(head, axis, [((i + 1) % count, i) for i in range(count)]),
            ],
            axis=dim,
        )
    return cells


def passed_along(value, axis, steps):
    count = lax.axis_size(axis)
    pairs = [(source, (source + steps) % count) for source in range(count)]
    return lax.ppermute(value, axis, pairs)


def normed(preact, scales):
    average = jnp.mean(preact, axis=-1, keepdims=True)
    centred = preact - average
    spread = jnp.mean(centred * centred, axis=-1, keepdims=True)
    return centred * lax.rsqrt(spread + 1e-05) * scales.astype(jnp.float32)


def finish(preact, project_out, scales):
    hidden = jax.nn.silu(preact).astype(jnp.bfloat16)
    return normed(jnp.dot(hidden, project_out, preferred_element_type=jnp.float32), scales)


def summed(targets, messages, node_count):
    onehot = (lax.iota(jnp.int32, node_count)[:, None] == targets[None, :]).astype(jnp.bfloat16)
    return jnp.dot(onehot, messages, preferred_element_type=jnp.float32)


def node_update(states, incoming, update_in, update_out, update_gain):
    features = states.shape[1]
    preact = jnp.dot(states, update_in[:features], preferred_element_type=jnp.float32)
    preact = preact + jnp.dot(
        incoming.astype(jnp.bfloat16), update_in[features:], preferred_element_type=jnp.float32
    )
    return (states.astype(jnp.float32) + finish(preact, update_out, update_gain)).astype(
        jnp.bfloat16
    )


def extend_rows(owned_rows, rim_count):
    rims = padded(owned_rows[:rim_count][None, None], (("gx", 0), ("gy", 1)), 1)
    return jnp.concatenate([owned_rows, rims.reshape(-1, owned_rows.shape[1])], axis=0)


def lift_rows(coarse_rows, rim_count, parents):
    rims = padded(coarse_rows[:rim_count][None, None], (("gx", 0), ("gy", 1)), 1)
    extended = jnp.concatenate([coarse_rows, rims.reshape(-1, coarse_rows.shape[1])], axis=0)
    return jnp.take(extended, parents, axis=0).astype(jnp.float32)


def coarse_level(
    owned_rows,
    extended,
    sources,
    targets,
    message_in,
    message_out,
    message_gain,
    update_in,
    update_out,
    update_gain,
):
    features = owned_rows.shape[1]
    source_proj = jnp.dot(extended, message_in[:features], preferred_element_type=jnp.float32)
    target_proj = jnp.dot(owned_rows, message_in[features:], preferred_element_type=jnp.float32)
    preact = jnp.take(source_proj, sources, axis=0) + jnp.take(target_proj, targets, axis=0)
    messages = finish(preact, message_out, message_gain).astype(jnp.bfloat16)
    incoming = summed(targets, messages, owned_rows.shape[0])
    return node_update(owned_rows, incoming, update_in, update_out, update_gain)


def restrict(states, parents, weights, local_count, rim_count):
    features = states.shape[1]
    positions = lax.iota(jnp.int32, local_count + 9 * rim_count)
    spread_matrix = jnp.where(
        positions[:, None] == parents[None, :], weights[None, :], jnp.zeros((), jnp.bfloat16)
    )
    spread_sums = jnp.dot(spread_matrix, states, preferred_element_type=jnp.float32)
    blocks = spread_sums[local_count:].reshape(3, 3, rim_count, features)
    column = blocks[1]
    for step_x in (-1, 1):
        column = column + passed_along(
            blocks[step_x + 1].astype(jnp.bfloat16), "gx", step_x
        ).astype(jnp.float32)
    inbound = column[1]
    for step_y in (-1, 1):
        inbound = inbound + passed_along(
            column[step_y + 1].astype(jnp.bfloat16), "gy", step_y
        ).astype(jnp.float32)
    owned = jnp.concatenate(
        [spread_sums[:rim_count] + inbound, spread_sums[rim_count:local_count]], axis=0
    )
    return owned.astype(jnp.bfloat16)


def per_device(
    fine_nodes,
    edge_latent,
    boundary,
    fine_src,
    fine_dst,
    parent_one,
    weight_one,
    coarse_src_one,
    coarse_dst_one,
    parent_two,
    weight_two,
    coarse_src_two,
    coarse_dst_two,
    fine_message_in,
    fine_message_out,
    fine_message_gain,
    fine_update_in,
    fine_update_out,
    fine_update_gain,
    coarse_message_in,
    coarse_message_out,
    coarse_message_gain,
    coarse_update_in,
    coarse_update_out,
    coarse_update_gain,
):
    features = fine_nodes.shape[1]
    edge_rows = jnp.take(fine_nodes, boundary, axis=0)
    beside_all = padded(edge_rows[None, None], (("gx", 0), ("gy", 1)), 1)
    source_weights = fine_message_in[:features]
    own_proj = jnp.dot(fine_nodes, source_weights, preferred_element_type=jnp.float32)
    target_proj = jnp.dot(
        fine_nodes, fine_message_in[features : 2 * features], preferred_element_type=jnp.float32
    )
    latent_proj = jnp.dot(
        edge_latent, fine_message_in[2 * features :], preferred_element_type=jnp.float32
    )
    around_proj = jnp.dot(
        beside_all.reshape(-1, features), source_weights, preferred_element_type=jnp.float32
    )
    source_proj = jnp.concatenate([own_proj, around_proj], axis=0)
    preact = (
        jnp.take(source_proj, fine_src, axis=0)
        + jnp.take(target_proj, fine_dst, axis=0)
        + latent_proj
    )
    messages = finish(preact, fine_message_out, fine_message_gain).astype(jnp.bfloat16)
    incoming = summed(fine_dst, messages, fine_nodes.shape[0])
    fine_new = node_update(fine_nodes, incoming, fine_update_in, fine_update_out, fine_update_gain)
    level_one = restrict(fine_new, parent_one, weight_one, NC1_DEV, CB1)
    level_one_new = coarse_level(
        level_one,
        extend_rows(level_one, CB1),
        coarse_src_one,
        coarse_dst_one,
        coarse_message_in,
        coarse_message_out,
        coarse_message_gain,
        coarse_update_in,
        coarse_update_out,
        coarse_update_gain,
    )
    level_two = restrict(level_one_new, parent_two, weight_two, NC2_DEV, CB2)
    level_two_new = coarse_level(
        level_two,
        extend_rows(level_two, CB2),
        coarse_src_two,
        coarse_dst_two,
        coarse_message_in,
        coarse_message_out,
        coarse_message_gain,
        coarse_update_in,
        coarse_update_out,
        coarse_update_gain,
    )
    level_one_final = (
        level_one_new.astype(jnp.float32) + lift_rows(level_two_new, CB2, parent_two)
    ).astype(jnp.bfloat16)
    return (fine_new.astype(jnp.float32) + lift_rows(level_one_final, CB1, parent_one)).astype(
        jnp.bfloat16
    )


def solution(mesh):
    in_specs = (
        P(("gx", "gy"), None),
        P(("gx", "gy"), None),
        P(("gx", "gy")),
        P(("gx", "gy")),
        P(("gx", "gy")),
        P(("gx", "gy")),
        P(("gx", "gy")),
        P(("gx", "gy")),
        P(("gx", "gy")),
        P(("gx", "gy")),
        P(("gx", "gy")),
        P(("gx", "gy")),
        P(("gx", "gy")),
        P(),
        P(),
        P(),
        P(),
        P(),
        P(),
        P(),
        P(),
        P(),
        P(),
        P(),
        P(),
    )
    out_specs = P(("gx", "gy"), None)
    return jax.shard_map(
        per_device, mesh=mesh, in_specs=in_specs, out_specs=out_specs, check_vma=False
    )
```

profile of v0, /device:TPU:1, one launch (start us, length us, event | category | flops | bytes accessed | tf_op | source)
XLA Modules:
  0.0 258.3 jit_solution(16888979611688780592)
XLA Ops:
  5.9 5.0 %collective-permute-start.1 = (bf16[1,1,128,512]{3,2,1,0:T(8,128)(2,1)S(1)}, bf16[1,1,128,512]{3,2,1,0:T(8,128)(2,1)S(1)}, u32[]{:S(2)}, u32[]{:S(2)}) collective-permute-start(bf16[1,1,128,512]{3,2,1,0:T(8,128)(2,1)S(1)} %bitcast_select_fusion), channel_id=1, source_target_pairs={{8,0},{16,8},{24,16},{32,24},{40,32},{48,40},{56,48},{64,56},{72,6... | collective-permute-start | bytes 393224 | tf_op jit(solution)/shard_map/ppermute | solution.py:21
  10.9 3.4 %fusion.53 = f32[1024,512]{1,0:T(8,128)} fusion(bf16[1024,512]{1,0:T(8,128)(2,1)} %param.25, bf16[1536,512]{1,0:T(8,128)(2,1)} %param.38), kind=kOutput, calls=%fused_computation.87 | convolution fusion | flops 536870912 | bytes 3670016 | tf_op jit(solution)/shard_map/dot_general | solution.py:149
  21.4 24.7 %gather_fusion.2 = f32[6144,512]{1,0:T(8,128)} fusion(f32[1024,512]{1,0:T(8,128)S(1)} %fusion.34, s32[6144]{0:T(1024)S(1)} %fusion.86), kind=kCustom, calls=%fused_computation.2 | custom fusion | bytes 25190400 | tf_op jit(solution)/shard_map/jit(_take)/gather | solution.py:162
  50.9 2.6 %collective-permute-done.2 = bf16[3,1,128,512]{3,2,1,0:T(8,128)(2,1)S(1)} collective-permute-done((bf16[3,1,128,512]{3,2,1,0:T(8,128)(2,1)S(1)}, bf16[3,1,128,512]{3,2,1,0:T(8,128)(2,1)S(1)}, u32[]{:S(2)}, u32[]{:S(2)}) %collective-permute-start.2) | collective-permute-done | bytes 393248 | tf_op jit(solution)/shard_map/ppermute | solution.py:19
  60.7 28.8 %gather_fusion.1 = f32[6144,512]{1,0:T(8,128)} fusion(f32[2176,512]{1,0:T(8,128)} %pad_maximum_fusion, s32[6144]{0:T(1024)S(1)} %fusion.85), kind=kCustom, calls=%fused_computation.1 | custom fusion | bytes 25190400 | tf_op jit(solution)/shard_map/jit(_take)/gather | solution.py:161
  89.4 20.9 %fusion.106 = (f32[6144]{0:T(1024)S(1)}, f32[6144,512]{0,1:T(8,128)}) fusion(bf16[512,512]{1,0:T(8,128)(2,1)S(1)} %copy-done, f32[6144,512]{1,0:T(8,128)} %gather_fusion.2, f32[6144,512]{1,0:T(8,128)} %gather_fusion.1, bf16[6144,512]{1,0:T(8,128)(2,1)} %param.26, pred[6144]{0:T(1024)(128)(4,1)S(1)} %get-tuple-element.34, ...), kind=kOutput, calls=%fused_computation.195 | convolution fusion | flops 6473902080 | bytes 45125632 | tf_op jit(solution)/shard_map/dot_general | solution.py:43
  110.4 6.1 %multiply_reduce_fusion = f32[6144]{0:T(1024)S(1)} fusion(f32[6144,512]{0,1:T(8,128)} %get-tuple-element.19, f32[6144]{0:T(1024)S(1)} %broadcast_multiply_fusion), kind=kLoop, calls=%fused_computation.12 | loop fusion | flops 9431040 | bytes 12632064 | tf_op jit(solution)/shard_map/reduce_sum | solution.py:37
  116.5 15.7 %multiply_convert_fusion.5 = bf16[1024,512]{1,0:T(8,128)(2,1)} fusion(f32[1024,512]{1,0:T(8,128)S(1)} %fusion.36, f32[6144,512]{0,1:T(8,128)} %get-tuple-element.19, f32[512]{0:T(512)S(1)} %convert_element_type.149, f32[6144]{0:T(1024)S(1)} %add_rsqrt_fusion, f32[6144]{0:T(1024)S(1)} %broadcast_multiply_fusion, s32[6144]{0:T(1024)S(1)} %copy-done.16, ...), kind=kOutput, calls=%fused_computation.32 | convolution fusion | flops 7001866240 | bytes 16328704 | tf_op jit(solution)/shard_map/dot_general | solution.py:54
  138.6 4.0 %collective-permute-done.4 = bf16[3,64,512]{2,1,0:T(8,128)(2,1)S(1)} collective-permute-done((bf16[3,64,512]{2,1,0:T(8,128)(2,1)S(1)}, bf16[3,64,512]{2,1,0:T(8,128)(2,1)S(1)}, u32[]{:S(2)}, u32[]{:S(2)}) %collective-permute-start.4) | collective-permute-done | bytes 196640 | tf_op jit(solution)/shard_map/ppermute | solution.py:31
  142.7 4.7 %collective-permute-done.5 = bf16[3,64,512]{2,1,0:T(8,128)(2,1)S(1)} collective-permute-done((bf16[3,64,512]{2,1,0:T(8,128)(2,1)S(1)}, bf16[3,64,512]{2,1,0:T(8,128)(2,1)S(1)}, u32[]{:S(2)}, u32[]{:S(2)}) %collective-permute-start.5) | collective-permute-done | bytes 196640 | tf_op jit(solution)/shard_map/ppermute | solution.py:31
  151.4 4.8 %collective-permute-start.9 = (bf16[1,1,64,512]{3,2,1,0:T(8,128)(2,1)S(1)}, bf16[1,1,64,512]{3,2,1,0:T(8,128)(2,1)S(1)}, u32[]{:S(2)}, u32[]{:S(2)}) collective-permute-start(bf16[1,1,64,512]{3,2,1,0:T(8,128)(2,1)S(1)} %bitcast.65), channel_id=1, source_target_pairs={{8,0},{16,8},{24,16},{32,24},{40,32},{48,40},{56,48},{64,56},{72,6... | collective-permute-start | bytes 196616 | tf_op jit(solution)/shard_map/ppermute | solution.py:21
  156.5 5.2 %gather_fusion.4 = f32[1536,512]{1,0:T(8,128)} fusion(f32[256,512]{1,0:T(8,128)S(1)} %fusion.42, s32[2048]{0:T(1024)S(1)} %pad_clamp_fusion), kind=kCustom, calls=%fused_computation.4 | custom fusion | bytes 6297600 | tf_op jit(solution)/shard_map/jit(_take)/gather | solution.py:88
  169.7 5.0 %gather_fusion.3 = f32[1536,512]{1,0:T(8,128)} fusion(f32[832,512]{1,0:T(8,128)S(1)} %fusion.21, s32[2048]{0:T(1024)S(1)} %pad_clamp_fusion.1), kind=kCustom, calls=%fused_computation.3 | custom fusion | bytes 6297600 | tf_op jit(solution)/shard_map/jit(_take)/gather | solution.py:88
  174.7 4.9 %fusion.111 = (f32[1536]{0:T(1024)S(1)}, f32[1536,512]{0,1:T(8,128)S(1)}) fusion(bf16[512,512]{1,0:T(8,128)(2,1)} %param.45, f32[1536,512]{1,0:T(8,128)} %gather_fusion.4, f32[1536,512]{1,0:T(8,128)} %gather_fusion.3, pred[1536]{0:T(1024)(128)(4,1)S(1)} %copy-done.31, pred[1536]{0:T(1024)(128)(4,1)S(1)} %copy-done.32), kind=kOutput, calls=%fused_computation.198 | convolution fusion | flops 812382720 | bytes 9970688 | tf_op jit(solution)/shard_map/dot_general | solution.py:43
  181.7 3.1 %multiply_convert_fusion.18 = bf16[256,512]{1,0:T(8,128)(2,1)S(1)} fusion(f32[256,512]{1,0:T(8,128)S(1)} %fusion.49, f32[1536,512]{0,1:T(8,128)} %copy-done.6, f32[512]{0:T(512)S(1)} %copy-done.33, f32[1536]{0:T(1024)S(1)} %add_rsqrt_fusion.1, f32[1536]{0:T(1024)S(1)} %broadcast_multiply_fusion.1, s32[1536]{0:T(1024)S(1)} %copy-done.19, ...), kind=kOutput, calls=%fused_computation.65 | convolution fusion | flops 541327360 | bytes 4476928 | tf_op jit(solution)/shard_map/dot_general | solution.py:54
  189.5 5.1 %collective-permute-done.13 = bf16[3,32,512]{2,1,0:T(8,128)(2,1)S(1)} collective-permute-done((bf16[3,32,512]{2,1,0:T(8,128)(2,1)S(1)}, bf16[3,32,512]{2,1,0:T(8,128)(2,1)S(1)}, u32[]{:S(2)}, u32[]{:S(2)}) %collective-permute-start.13) | collective-permute-done | bytes 98336 | tf_op jit(solution)/shard_map/ppermute | solution.py:31
  194.7 5.2 %collective-permute-start.14 = (bf16[32,512]{1,0:T(8,128)(2,1)S(1)}, bf16[32,512]{1,0:T(8,128)(2,1)S(1)}, u32[]{:S(2)}, u32[]{:S(2)}) collective-permute-start(bf16[32,512]{1,0:T(8,128)(2,1)S(1)} %get-tuple-element.16), channel_id=1, source_target_pairs={{0,7},{1,0},{2,1},{3,2},{4,3},{5,4},{6,5},{7,6},{8,15},{9,8},{10,9... | collective-permute-start | bytes 98312 | tf_op jit(solution)/shard_map/ppermute | solution.py:31
  202.2 4.8 %collective-permute-start.17 = (bf16[1,1,32,512]{3,2,1,0:T(8,128)(2,1)S(1)}, bf16[1,1,32,512]{3,2,1,0:T(8,128)(2,1)S(1)}, u32[]{:S(2)}, u32[]{:S(2)}) collective-permute-start(bf16[1,1,32,512]{3,2,1,0:T(8,128)(2,1)S(1)} %bitcast.72), channel_id=1, source_target_pairs={{8,0},{16,8},{24,16},{32,24},{40,32},{48,40},{56,48},{64,56},{72,6... | collective-permute-start | bytes 98312 | tf_op jit(solution)/shard_map/ppermute | solution.py:21
  210.6 2.8 %collective-permute-start.19 = (bf16[3,1,32,512]{3,2,1,0:T(8,128)(2,1)S(1)}, bf16[3,1,32,512]{3,2,1,0:T(8,128)(2,1)S(1)}, u32[]{:S(2)}, u32[]{:S(2)}) collective-permute-start(bf16[3,1,32,512]{3,2,1,0:T(8,128)(2,1)S(1)} %pad_maximum_fusion.12), channel_id=1, source_target_pairs={{1,0},{2,1},{3,2},{4,3},{5,4},{6,5},{7,6},{0,7},{9,8},{10,9},{11,1... | collective-permute-start | bytes 294920 | tf_op jit(solution)/shard_map/ppermute | solution.py:21
  225.0 5.1 %collective-permute-start.21 = (bf16[1,1,32,512]{3,2,1,0:T(8,128)(2,1)S(1)}, bf16[1,1,32,512]{3,2,1,0:T(8,128)(2,1)S(1)}, u32[]{:S(2)}, u32[]{:S(2)}) collective-permute-start(bf16[1,1,32,512]{3,2,1,0:T(8,128)(2,1)S(1)} %slice_bitcast_fusion.5), channel_id=1, source_target_pairs={{8,0},{16,8},{24,16},{32,24},{40,32},{48,40},{56,48},{64,56},{72,6... | collective-permute-start | bytes 98312 | tf_op jit(solution)/shard_map/ppermute | solution.py:21
  231.4 3.8 %collective-permute-start.23 = (bf16[3,1,32,512]{3,2,1,0:T(8,128)(2,1)S(1)}, bf16[3,1,32,512]{3,2,1,0:T(8,128)(2,1)S(1)}, u32[]{:S(2)}, u32[]{:S(2)}) collective-permute-start(bf16[3,1,32,512]{3,2,1,0:T(8,128)(2,1)S(1)} %pad_maximum_fusion.13), channel_id=1, source_target_pairs={{1,0},{2,1},{3,2},{4,3},{5,4},{6,5},{7,6},{0,7},{9,8},{10,9},{11,1... | collective-permute-start | bytes 294920 | tf_op jit(solution)/shard_map/ppermute | solution.py:21
  237.6 5.2 %collective-permute-start.25 = (bf16[1,1,64,512]{3,2,1,0:T(8,128)(2,1)S(1)}, bf16[1,1,64,512]{3,2,1,0:T(8,128)(2,1)S(1)}, u32[]{:S(2)}, u32[]{:S(2)}) collective-permute-start(bf16[1,1,64,512]{3,2,1,0:T(8,128)(2,1)S(1)} %slice_bitcast_fusion.1), channel_id=1, source_target_pairs={{8,0},{16,8},{24,16},{32,24},{40,32},{48,40},{56,48},{64,56},{72,6... | collective-permute-start | bytes 196616 | tf_op jit(solution)/shard_map/ppermute | solution.py:21
  244.5 5.1 %collective-permute-start.27 = (bf16[3,1,64,512]{3,2,1,0:T(8,128)(2,1)S(1)}, bf16[3,1,64,512]{3,2,1,0:T(8,128)(2,1)S(1)}, u32[]{:S(2)}, u32[]{:S(2)}) collective-permute-start(bf16[3,1,64,512]{3,2,1,0:T(8,128)(2,1)S(1)} %pad_maximum_fusion.11), channel_id=1, source_target_pairs={{1,0},{2,1},{3,2},{4,3},{5,4},{6,5},{7,6},{0,7},{9,8},{10,9},{11,1... | collective-permute-start | bytes 589832 | tf_op jit(solution)/shard_map/ppermute | solution.py:21
  250.8 4.0 %gather_fusion.8 = bf16[1024,512]{1,0:T(8,128)(2,1)S(1)} fusion(bf16[832,512]{1,0:T(8,128)(2,1)S(1)} %pad_maximum_fusion.2, s32[1024]{0:T(1024)S(1)} %fusion.87), kind=kCustom, calls=%fused_computation.8 | custom fusion | bytes 2101248 | tf_op jit(solution)/shard_map/jit(_take)/gather | solution.py:70
  (224 shorter events, 77.4 us)
Async XLA Ops:
  3.8 43.0 %collective-permute-start = (bf16[1,1,128,512]{3,2,1,0:T(8,128)(2,1)S(1)}, bf16[1,1,128,512]{3,2,1,0:T(8,128)(2,1)S(1)}, u32[]{:S(2)}, u32[]{:S(2)}) collective-permute-start(bf16[1,1,128,512]{3,2,1,0:T(8,128)(2,1)S(1)} %bitcast_select_fusion), channel_id=1, source_target_pairs={{0,8},{8,16},{16,24},{24,32},{32,40},{40,48},{48,56},{56,64},{64,7... | collective-permute-start | bytes 393224 | tf_op jit(solution)/shard_map/ppermute | solution.py:19
  5.9 40.8 %collective-permute-start.1 = (bf16[1,1,128,512]{3,2,1,0:T(8,128)(2,1)S(1)}, bf16[1,1,128,512]{3,2,1,0:T(8,128)(2,1)S(1)}, u32[]{:S(2)}, u32[]{:S(2)}) collective-permute-start(bf16[1,1,128,512]{3,2,1,0:T(8,128)(2,1)S(1)} %bitcast_select_fusion), channel_id=1, source_target_pairs={{8,0},{16,8},{24,16},{32,24},{40,32},{48,40},{56,48},{64,56},{72,6... | collective-permute-start | bytes 393224 | tf_op jit(solution)/shard_map/ppermute | solution.py:21
  46.8 6.8 %collective-permute-start.2 = (bf16[3,1,128,512]{3,2,1,0:T(8,128)(2,1)S(1)}, bf16[3,1,128,512]{3,2,1,0:T(8,128)(2,1)S(1)}, u32[]{:S(2)}, u32[]{:S(2)}) collective-permute-start(bf16[3,1,128,512]{3,2,1,0:T(8,128)(2,1)S(1)} %pad_maximum_fusion.5), channel_id=1, source_target_pairs={{0,1},{1,2},{2,3},{3,4},{4,5},{5,6},{6,7},{7,0},{8,9},{9,10},{10,1... | collective-permute-start | bytes 1179656 | tf_op jit(solution)/shard_map/ppermute | solution.py:19
  48.9 7.2 %collective-permute-start.3 = (bf16[3,1,128,512]{3,2,1,0:T(8,128)(2,1)S(1)}, bf16[3,1,128,512]{3,2,1,0:T(8,128)(2,1)S(1)}, u32[]{:S(2)}, u32[]{:S(2)}) collective-permute-start(bf16[3,1,128,512]{3,2,1,0:T(8,128)(2,1)S(1)} %pad_maximum_fusion.5), channel_id=1, source_target_pairs={{1,0},{2,1},{3,2},{4,3},{5,4},{6,5},{7,6},{0,7},{9,8},{10,9},{11,1... | collective-permute-start | bytes 1179656 | tf_op jit(solution)/shard_map/ppermute | solution.py:21
  136.2 6.4 %collective-permute-start.4 = (bf16[3,64,512]{2,1,0:T(8,128)(2,1)S(1)}, bf16[3,64,512]{2,1,0:T(8,128)(2,1)S(1)}, u32[]{:S(2)}, u32[]{:S(2)}) collective-permute-start(bf16[3,64,512]{2,1,0:T(8,128)(2,1)S(1)} %bitcast.79), channel_id=1, source_target_pairs={{0,120},{8,0},{16,8},{24,16},{32,24},{40,32},{48,40},{56,48},{64,5... | collective-permute-start | bytes 589832 | tf_op jit(solution)/shard_map/ppermute | solution.py:31
  138.0 9.4 %collective-permute-start.5 = (bf16[3,64,512]{2,1,0:T(8,128)(2,1)S(1)}, bf16[3,64,512]{2,1,0:T(8,128)(2,1)S(1)}, u32[]{:S(2)}, u32[]{:S(2)}) collective-permute-start(bf16[3,64,512]{2,1,0:T(8,128)(2,1)S(1)} %bitcast.78), channel_id=1, source_target_pairs={{0,8},{8,16},{16,24},{24,32},{32,40},{40,48},{48,56},{56,64},{64,7... | collective-permute-start | bytes 589832 | tf_op jit(solution)/shard_map/ppermute | solution.py:31
  151.3 10.3 %collective-permute-start.8 = (bf16[1,1,64,512]{3,2,1,0:T(8,128)(2,1)S(1)}, bf16[1,1,64,512]{3,2,1,0:T(8,128)(2,1)S(1)}, u32[]{:S(2)}, u32[]{:S(2)}) collective-permute-start(bf16[1,1,64,512]{3,2,1,0:T(8,128)(2,1)S(1)} %bitcast.64), channel_id=1, source_target_pairs={{0,8},{8,16},{16,24},{24,32},{32,40},{40,48},{48,56},{56,64},{64,7... | collective-permute-start | bytes 196616 | tf_op jit(solution)/shard_map/ppermute | solution.py:19
  151.4 10.3 %collective-permute-start.9 = (bf16[1,1,64,512]{3,2,1,0:T(8,128)(2,1)S(1)}, bf16[1,1,64,512]{3,2,1,0:T(8,128)(2,1)S(1)}, u32[]{:S(2)}, u32[]{:S(2)}) collective-permute-start(bf16[1,1,64,512]{3,2,1,0:T(8,128)(2,1)S(1)} %bitcast.65), channel_id=1, source_target_pairs={{8,0},{16,8},{24,16},{32,24},{40,32},{48,40},{56,48},{64,56},{72,6... | collective-permute-start | bytes 196616 | tf_op jit(solution)/shard_map/ppermute | solution.py:21
  161.7 5.7 %collective-permute-start.10 = (bf16[3,1,64,512]{3,2,1,0:T(8,128)(2,1)S(1)}, bf16[3,1,64,512]{3,2,1,0:T(8,128)(2,1)S(1)}, u32[]{:S(2)}, u32[]{:S(2)}) collective-permute-start(bf16[3,1,64,512]{3,2,1,0:T(8,128)(2,1)S(1)} %pad_maximum_fusion.10), channel_id=1, source_target_pairs={{0,1},{1,2},{2,3},{3,4},{4,5},{5,6},{6,7},{7,0},{8,9},{9,10},{10,1... | collective-permute-start | bytes 589832 | tf_op jit(solution)/shard_map/ppermute | solution.py:19
  163.9 5.1 %collective-permute-start.11 = (bf16[3,1,64,512]{3,2,1,0:T(8,128)(2,1)S(1)}, bf16[3,1,64,512]{3,2,1,0:T(8,128)(2,1)S(1)}, u32[]{:S(2)}, u32[]{:S(2)}) collective-permute-start(bf16[3,1,64,512]{3,2,1,0:T(8,128)(2,1)S(1)} %pad_maximum_fusion.10), channel_id=1, source_target_pairs={{1,0},{2,1},{3,2},{4,3},{5,4},{6,5},{7,6},{0,7},{9,8},{10,9},{11,1... | collective-permute-start | bytes 589832 | tf_op jit(solution)/shard_map/ppermute | solution.py:21
  187.9 6.8 %collective-permute-start.13 = (bf16[3,32,512]{2,1,0:T(8,128)(2,1)S(1)}, bf16[3,32,512]{2,1,0:T(8,128)(2,1)S(1)}, u32[]{:S(2)}, u32[]{:S(2)}) collective-permute-start(bf16[3,32,512]{2,1,0:T(8,128)(2,1)S(1)} %bitcast.80), channel_id=1, source_target_pairs={{0,8},{8,16},{16,24},{24,32},{32,40},{40,48},{48,56},{56,64},{64,7... | collective-permute-start | bytes 294920 | tf_op jit(solution)/shard_map/ppermute | solution.py:31
  194.7 6.0 %collective-permute-start.14 = (bf16[32,512]{1,0:T(8,128)(2,1)S(1)}, bf16[32,512]{1,0:T(8,128)(2,1)S(1)}, u32[]{:S(2)}, u32[]{:S(2)}) collective-permute-start(bf16[32,512]{1,0:T(8,128)(2,1)S(1)} %get-tuple-element.16), channel_id=1, source_target_pairs={{0,7},{1,0},{2,1},{3,2},{4,3},{5,4},{6,5},{7,6},{8,15},{9,8},{10,9... | collective-permute-start | bytes 98312 | tf_op jit(solution)/shard_map/ppermute | solution.py:31
  202.2 6.2 %collective-permute-start.16 = (bf16[1,1,32,512]{3,2,1,0:T(8,128)(2,1)S(1)}, bf16[1,1,32,512]{3,2,1,0:T(8,128)(2,1)S(1)}, u32[]{:S(2)}, u32[]{:S(2)}) collective-permute-start(bf16[1,1,32,512]{3,2,1,0:T(8,128)(2,1)S(1)} %bitcast.71), channel_id=1, source_target_pairs={{0,8},{8,16},{16,24},{24,32},{32,40},{40,48},{48,56},{56,64},{64,7... | collective-permute-start | bytes 98312 | tf_op jit(solution)/shard_map/ppermute | solution.py:19
  202.2 6.1 %collective-permute-start.17 = (bf16[1,1,32,512]{3,2,1,0:T(8,128)(2,1)S(1)}, bf16[1,1,32,512]{3,2,1,0:T(8,128)(2,1)S(1)}, u32[]{:S(2)}, u32[]{:S(2)}) collective-permute-start(bf16[1,1,32,512]{3,2,1,0:T(8,128)(2,1)S(1)} %bitcast.72), channel_id=1, source_target_pairs={{8,0},{16,8},{24,16},{32,24},{40,32},{48,40},{56,48},{64,56},{72,6... | collective-permute-start | bytes 98312 | tf_op jit(solution)/shard_map/ppermute | solution.py:21
  208.3 8.1 %collective-permute-start.18 = (bf16[3,1,32,512]{3,2,1,0:T(8,128)(2,1)S(1)}, bf16[3,1,32,512]{3,2,1,0:T(8,128)(2,1)S(1)}, u32[]{:S(2)}, u32[]{:S(2)}) collective-permute-start(bf16[3,1,32,512]{3,2,1,0:T(8,128)(2,1)S(1)} %pad_maximum_fusion.12), channel_id=1, source_target_pairs={{0,1},{1,2},{2,3},{3,4},{4,5},{5,6},{6,7},{7,0},{8,9},{9,10},{10,1... | collective-permute-start | bytes 294920 | tf_op jit(solution)/shard_map/ppermute | solution.py:19
  210.6 5.9 %collective-permute-start.19 = (bf16[3,1,32,512]{3,2,1,0:T(8,128)(2,1)S(1)}, bf16[3,1,32,512]{3,2,1,0:T(8,128)(2,1)S(1)}, u32[]{:S(2)}, u32[]{:S(2)}) collective-permute-start(bf16[3,1,32,512]{3,2,1,0:T(8,128)(2,1)S(1)} %pad_maximum_fusion.12), channel_id=1, source_target_pairs={{1,0},{2,1},{3,2},{4,3},{5,4},{6,5},{7,6},{0,7},{9,8},{10,9},{11,1... | collective-permute-start | bytes 294920 | tf_op jit(solution)/shard_map/ppermute | solution.py:21
  224.9 6.4 %collective-permute-start.20 = (bf16[1,1,32,512]{3,2,1,0:T(8,128)(2,1)S(1)}, bf16[1,1,32,512]{3,2,1,0:T(8,128)(2,1)S(1)}, u32[]{:S(2)}, u32[]{:S(2)}) collective-permute-start(bf16[1,1,32,512]{3,2,1,0:T(8,128)(2,1)S(1)} %slice_bitcast_fusion.5), channel_id=1, source_target_pairs={{0,8},{8,16},{16,24},{24,32},{32,40},{40,48},{48,56},{56,64},{64,7... | collective-permute-start | bytes 98312 | tf_op jit(solution)/shard_map/ppermute | solution.py:19
  225.0 6.4 %collective-permute-start.21 = (bf16[1,1,32,512]{3,2,1,0:T(8,128)(2,1)S(1)}, bf16[1,1,32,512]{3,2,1,0:T(8,128)(2,1)S(1)}, u32[]{:S(2)}, u32[]{:S(2)}) collective-permute-start(bf16[1,1,32,512]{3,2,1,0:T(8,128)(2,1)S(1)} %slice_bitcast_fusion.5), channel_id=1, source_target_pairs={{8,0},{16,8},{24,16},{32,24},{40,32},{48,40},{56,48},{64,56},{72,6... | collective-permute-start | bytes 98312 | tf_op jit(solution)/shard_map/ppermute | solution.py:21
  231.3 4.6 %collective-permute-start.22 = (bf16[3,1,32,512]{3,2,1,0:T(8,128)(2,1)S(1)}, bf16[3,1,32,512]{3,2,1,0:T(8,128)(2,1)S(1)}, u32[]{:S(2)}, u32[]{:S(2)}) collective-permute-start(bf16[3,1,32,512]{3,2,1,0:T(8,128)(2,1)S(1)} %pad_maximum_fusion.13), channel_id=1, source_target_pairs={{0,1},{1,2},{2,3},{3,4},{4,5},{5,6},{6,7},{7,0},{8,9},{9,10},{10,1... | collective-permute-start | bytes 294920 | tf_op jit(solution)/shard_map/ppermute | solution.py:19
  231.4 4.8 %collective-permute-start.23 = (bf16[3,1,32,512]{3,2,1,0:T(8,128)(2,1)S(1)}, bf16[3,1,32,512]{3,2,1,0:T(8,128)(2,1)S(1)}, u32[]{:S(2)}, u32[]{:S(2)}) collective-permute-start(bf16[3,1,32,512]{3,2,1,0:T(8,128)(2,1)S(1)} %pad_maximum_fusion.13), channel_id=1, source_target_pairs={{1,0},{2,1},{3,2},{4,3},{5,4},{6,5},{7,6},{0,7},{9,8},{10,9},{11,1... | collective-permute-start | bytes 294920 | tf_op jit(solution)/shard_map/ppermute | solution.py:21
  237.5 6.9 %collective-permute-start.24 = (bf16[1,1,64,512]{3,2,1,0:T(8,128)(2,1)S(1)}, bf16[1,1,64,512]{3,2,1,0:T(8,128)(2,1)S(1)}, u32[]{:S(2)}, u32[]{:S(2)}) collective-permute-start(bf16[1,1,64,512]{3,2,1,0:T(8,128)(2,1)S(1)} %slice_bitcast_fusion.1), channel_id=1, source_target_pairs={{0,8},{8,16},{16,24},{24,32},{32,40},{40,48},{48,56},{56,64},{64,7... | collective-permute-start | bytes 196616 | tf_op jit(solution)/shard_map/ppermute | solution.py:19
  237.6 6.8 %collective-permute-start.25 = (bf16[1,1,64,512]{3,2,1,0:T(8,128)(2,1)S(1)}, bf16[1,1,64,512]{3,2,1,0:T(8,128)(2,1)S(1)}, u32[]{:S(2)}, u32[]{:S(2)}) collective-permute-start(bf16[1,1,64,512]{3,2,1,0:T(8,128)(2,1)S(1)} %slice_bitcast_fusion.1), channel_id=1, source_target_pairs={{8,0},{16,8},{24,16},{32,24},{40,32},{48,40},{56,48},{64,56},{72,6... | collective-permute-start | bytes 196616 | tf_op jit(solution)/shard_map/ppermute | solution.py:21
  244.4 6.1 %collective-permute-start.26 = (bf16[3,1,64,512]{3,2,1,0:T(8,128)(2,1)S(1)}, bf16[3,1,64,512]{3,2,1,0:T(8,128)(2,1)S(1)}, u32[]{:S(2)}, u32[]{:S(2)}) collective-permute-start(bf16[3,1,64,512]{3,2,1,0:T(8,128)(2,1)S(1)} %pad_maximum_fusion.11), channel_id=1, source_target_pairs={{0,1},{1,2},{2,3},{3,4},{4,5},{5,6},{6,7},{7,0},{8,9},{9,10},{10,1... | collective-permute-start | bytes 589832 | tf_op jit(solution)/shard_map/ppermute | solution.py:19
  244.5 6.2 %collective-permute-start.27 = (bf16[3,1,64,512]{3,2,1,0:T(8,128)(2,1)S(1)}, bf16[3,1,64,512]{3,2,1,0:T(8,128)(2,1)S(1)}, u32[]{:S(2)}, u32[]{:S(2)}) collective-permute-start(bf16[3,1,64,512]{3,2,1,0:T(8,128)(2,1)S(1)} %pad_maximum_fusion.11), channel_id=1, source_target_pairs={{1,0},{2,1},{3,2},{4,3},{5,4},{6,5},{7,6},{0,7},{9,8},{10,9},{11,1... | collective-permute-start | bytes 589832 | tf_op jit(solution)/shard_map/ppermute | solution.py:21
  (46 other events, 366.9 us)
where the time goes:
time: 263 us; the launch traced here: 258 us
  local copies, waits for them, and re-layouts  82.4 us (31%)
  matrix products  64.2 us (24%)
  starting transfers between devices  58.8 us (22%)
  waiting for transfers between devices  33 us (13%)
  other arithmetic  18.9 us (7%)
    ppermute x10, starting transfers between devices, padded(): lax.ppermute(head, axis, [((i + 1) % count, i) for i in range(count)])  39.1 us
    dot_general x6, matrix products, finish(): jnp.dot(hidden, project_out, preferred_element_type=jnp.float32)  30.8 us
    gather x1, local copies, waits for them, and re-layouts, per_device(): jnp.take(source_proj, fine_src, axis=0)  28.8 us
    gather x1, local copies, waits for them, and re-layouts, per_device(): jnp.take(target_proj, fine_dst, axis=0)  24.7 us
    dot_general x3, matrix products, node_update(): jnp.dot(incoming.astype(jnp.bfloat16), update_in[features:], preferred_el...  20.5 us
    ppermute x8, waiting for transfers between devices, passed_along(): return lax.ppermute(value, axis, pairs)  19.8 us
    ppermute x8, starting transfers between devices, passed_along(): return lax.ppermute(value, axis, pairs)  10.6 us
    ppermute x10, starting transfers between devices, padded(): lax.ppermute(tail, axis, [(i, (i + 1) % count) for i in range(count)])  9.1 us
  transfers between devices with their start and end apart: 28, of which 19 were waited for; matrix products, arithmetic and copies ran while one was open for 18% of the time, Pallas kernels for 0%

commit v1 on v0

v1 whole, which is shorter than its diff:
```python
import jax
import jax.numpy as jnp
from jax import lax
from jax.experimental import pallas as pl
from jax.experimental.pallas import tpu as pltpu
from jax.sharding import PartitionSpec as P

MESH = pl.DeviceIdType.MESH
BF16 = jnp.bfloat16
F32 = jnp.float32

D = 512
NF = 1024
BND = 128
EDGES = 6144
N1, R1, E1 = 256, 64, 1536
N2, R2, E2 = 64, 32, 384
T1 = 512
T2 = 512
OFFSETS = [(k // 3 - 1, k % 3 - 1) for k in range(9) if k != 4]


def neighbours(n_gx, n_gy):
    ix, iy = lax.axis_index("gx"), lax.axis_index("gy")
    return [
        (lax.rem(ix + dx + n_gx, n_gx), lax.rem(iy + dy + n_gy, n_gy)) for dx, dy in OFFSETS
    ]


def greet(around):
    barrier = pltpu.get_barrier_semaphore()
    for who in around:
        pl.semaphore_signal(barrier, inc=1, device_id=who, device_id_type=MESH)


def all_greeted():
    pl.semaphore_wait(pltpu.get_barrier_semaphore(), 8)


def exchange(around, piece, landing, send_sem, recv_sem):
    copies = []
    for s, who in enumerate(around):
        copies.append(
            pltpu.make_async_remote_copy(
                src_ref=piece(s),
                dst_ref=landing.at[7 - s],
                send_sem=send_sem.at[s],
                recv_sem=recv_sem.at[7 - s],
                device_id=who,
                device_id_type=MESH,
            )
        )
    for copy in copies:
        copy.start()
    return copies


def finished(copies):
    for copy in copies:
        copy.wait()


def dot(a, b):
    return jnp.dot(a, b, preferred_element_type=F32)


def silu(v):
    half = 0.5 * v
    return half + half * jnp.tanh(half)


def normed(v, gain):
    centred = v - jnp.mean(v, axis=-1, keepdims=True)
    spread = jnp.mean(centred * centred, axis=-1, keepdims=True)
    return centred * lax.rsqrt(spread + 1e-05) * gain


def packed_numbers(numbers, local, rim):
    return jnp.where(numbers >= local + 5 * rim, numbers - rim, numbers)


def pick_rows(row, width, first=0):
    across = jnp.broadcast_to(row - first, (128, 128)).T
    lane = lax.broadcasted_iota(jnp.int32, (128, 128), 1)
    return jnp.concatenate(
        [
            jnp.where(across == lane + 128 * c, 1.0, 0.0).astype(BF16)
            for c in range(width // 128)
        ],
        axis=1,
    )


def pick_matrix(rows, start, count, width, first=0):
    return jnp.concatenate(
        [pick_rows(rows[:, start + j : start + j + 128], width, first) for j in range(0, count, 128)],
        axis=0,
    )


def gather_sums(rows, height):
    down = lax.broadcasted_iota(jnp.int32, (height, rows.shape[1]), 0)
    return jnp.where(down == rows, 1.0, 0.0).astype(BF16)


def halo_kernel(
    n_gx, n_gy, nodes, bnd, src, dst, latent, w_in, base, halo_out, src_out,
    target, edge_rows, halo, send_sem, recv_sem,
):
    step = pl.program_id(0)
    around = neighbours(n_gx, n_gy)

    @pl.when(step == 0)
    def _():
        greet(around)
        edge_rows[...] = dot(pick_rows(bnd[...], NF), nodes[...]).astype(BF16)
        all_greeted()
        exchange(around, lambda s: edge_rows, halo, send_sem, recv_sem)
        target[...] = dot(nodes[...], w_in[D : 2 * D]).astype(BF16)
        src_out[...] = packed_numbers(src[...], NF, BND) * 4

    base[...] = (
        dot(pick_matrix(dst[0], 0, T1, NF), target[...]) + dot(latent[...], w_in[2 * D :])
    ).astype(BF16)

    @pl.when(step == pl.num_programs(0) - 1)
    def _():
        for s, who in enumerate(around):
            pltpu.make_async_remote_copy(
                src_ref=edge_rows,
                dst_ref=halo.at[7 - s],
                send_sem=send_sem.at[s],
                recv_sem=recv_sem.at[7 - s],
                device_id=who,
                device_id_type=MESH,
            ).wait()
        for s in range(8):
            halo_out[pl.ds(s * BND, BND), :] = halo[s]


def edge_kernel(
    nodes, halo, src, dst, base, w_src, w_out, gain, up_in, up_out, up_gain, fine_new,
    table, picked, total,
):
    step = pl.program_id(0)

    def pick(first):
        for e in range(T2):
            row = pl.multiple_of(src[first + e], 4)
            picked[pl.ds(4 * e, 4), :] = table[pl.ds(row, 4), :]

    @pl.when(step == 0)
    def _():
        for c in range(0, 2 * NF, 256):
            rows = nodes[c : c + 256] if c < NF else halo[c - NF : c - NF + 256]
            value = dot(rows, w_src[...])
            for j in range(4):
                table[pl.ds(4 * c + j, 256, stride=4), :] = value[:, 128 * j : 128 * (j + 1)]
        total[...] = jnp.zeros_like(total)
        pick(0)

    source = jnp.concatenate(
        [picked[pl.ds(j, T2, stride=4), :] for j in range(4)], axis=1
    )
    hidden = silu(source + base[...].astype(F32)).astype(BF16)
    following = jnp.minimum(step + 1, pl.num_programs(0) - 1) * T2
    pick(following)
    messages = normed(dot(hidden, w_out[...]), gain[...].astype(F32)).astype(BF16)
    total[...] += dot(gather_sums(dst[0], NF), messages)

    @pl.when(step == pl.num_programs(0) - 1)
    def _():
        incoming = total[...].astype(BF16)
        states = nodes[...]
        update = silu(dot(states, up_in[:D]) + dot(incoming, up_in[D:])).astype(BF16)
        fine_new[...] = (
            states.astype(F32) + normed(dot(update, up_out[...]), up_gain[...].astype(F32))
        ).astype(BF16)


def spread_sums(states, parents, weights, local, rim):
    numbers = packed_numbers(parents, local, rim)
    down = lax.broadcasted_iota(jnp.int32, (local + 8 * rim, parents.shape[1]), 0)
    spread = jnp.where(down == numbers, weights.astype(F32), 0.0).astype(BF16)
    return dot(spread, states)


def node_update(states, incoming, up_in, up_out, up_gain):
    update = silu(dot(states, up_in[:D]) + dot(incoming, up_in[D:])).astype(BF16)
    return (
        states.astype(F32) + normed(dot(update, up_out[...]), up_gain[...].astype(F32))
    ).astype(BF16)


def coarse_kernel(
    n_gx, n_gy, fine, parent1, weight1, src1, dst1, parent2, weight2, src2, dst2,
    msg_in, msg_out, msg_gain, up_in, up_out, up_gain, out,
    sums1, land_a, level1, land_b, sums2, land_c, level2, land_d, new2, land_e, final1, land_f,
    preact, send_sem, recv_sem,
):
    around = neighbours(n_gx, n_gy)
    greet(around)

    def swap(i, piece, landing):
        return exchange(around, piece, landing, send_sem.at[i], recv_sem.at[i])

    parents = packed_numbers(parent1[...], N1, R1)
    spread = spread_sums(fine[...], parent1[...], weight1[...], N1, R1)
    sums1[...] = spread[N1:].astype(BF16)
    all_greeted()
    moving = swap(0, lambda s: sums1.at[pl.ds(s * R1, R1)], land_a)
    down_rows = gather_sums(dst1[...], N1)
    finished(moving)
    rim = spread[:R1]
    for s in range(8):
        rim = rim + land_a[s].astype(F32)
    level1[...] = jnp.concatenate([rim, spread[R1:N1]], axis=0).astype(BF16)

    moving = swap(1, lambda s: level1.at[pl.ds(0, R1)], land_b)
    own = dot(level1[...], msg_in[:D]).astype(BF16)
    mine = dot(level1[...], msg_in[D:]).astype(BF16)
    numbers = packed_numbers(src1[...], N1, R1)
    for t in range(0, E1, 512):
        preact[pl.ds(t, 512), :] = dot(pick_matrix(numbers, t, 512, N1), own) + dot(
            pick_matrix(dst1, t, 512, N1), mine
        )
    finished(moving)
    beyond = dot(land_b[...].reshape(8 * R1, D), msg_in[:D]).astype(BF16)
    incoming = jnp.zeros((N1, D), F32)
    for t in range(0, E1, 512):
        hidden = silu(
            preact[pl.ds(t, 512), :] + dot(pick_matrix(numbers, t, 512, 8 * R1, N1), beyond)
        ).astype(BF16)
        messages = normed(dot(hidden, msg_out[...]), msg_gain[...].astype(F32)).astype(BF16)
        incoming = incoming + dot(down_rows[:, t : t + 512], messages)
    new1 = node_update(level1[...], incoming.astype(BF16), up_in, up_out, up_gain)

    spread = spread_sums(new1, parent2[...], weight2[...], N2, R2)
    sums2[...] = spread[N2:].astype(BF16)
    moving = swap(2, lambda s: sums2.at[pl.ds(s * R2, R2)], land_c)
    finished(moving)
    rim = spread[:R2]
    for s in range(8):
        rim = rim + land_c[s].astype(F32)
    level2[...] = jnp.concatenate([rim, spread[R2:N2]], axis=0).astype(BF16)

    moving = swap(3, lambda s: level2.at[pl.ds(0, R2)], land_d)
    mine = dot(level2[...], msg_in[D:]).astype(BF16)
    own = dot(level2[...], msg_in[:D]).astype(BF16)
    numbers = packed_numbers(src2[...], N2, R2)
    pad = jnp.zeros((64, D), BF16)
    start = dot(pick_matrix(dst2, 0, E2, 128), jnp.concatenate([mine, pad], axis=0)) + dot(
        pick_matrix(numbers, 0, E2, 128), jnp.concatenate([own, pad], axis=0)
    )
    finished(moving)
    beyond = dot(land_d[...].reshape(8 * R2, D), msg_in[:D]).astype(BF16)
    hidden = silu(start + dot(pick_matrix(numbers, 0, E2, 8 * R2, N2), beyond)).astype(BF16)
    messages = normed(dot(hidden, msg_out[...]), msg_gain[...].astype(F32)).astype(BF16)
    incoming = dot(gather_sums(dst2[...], N2), messages).astype(BF16)
    new2[...] = node_update(level2[...], incoming, up_in, up_out, up_gain)

    moving = swap(4, lambda s: new2.at[pl.ds(0, R2)], land_e)
    numbers = packed_numbers(parent2[...], N2, R2)
    lift = new1.astype(F32) + dot(
        pick_matrix(numbers, 0, N1, 128), jnp.concatenate([new2[...], pad], axis=0)
    )
    finished(moving)
    final1[...] = (
        lift + dot(pick_matrix(numbers, 0, N1, 8 * R2, N2), land_e[...].reshape(8 * R2, D))
    ).astype(BF16)

    moving = swap(5, lambda s: final1.at[pl.ds(0, R1)], land_f)
    for t in range(0, NF, 512):
        preact[pl.ds(t, 512), :] = fine[pl.ds(t, 512), :].astype(F32) + dot(
            pick_matrix(parents, t, 512, N1), final1[...]
        )
    finished(moving)
    rims = land_f[...].reshape(8 * R1, D)
    for t in range(0, NF, 512):
        out[pl.ds(t, 512), :] = (
            preact[pl.ds(t, 512), :] + dot(pick_matrix(parents, t, 512, 8 * R1, N1), rims)
        ).astype(BF16)


def vmem():
    return pl.BlockSpec(memory_space=pltpu.VMEM)


def per_device(n_gx, n_gy, args):
    (
        fine_nodes, edge_latent, boundary, fine_src, fine_dst, parent_one, weight_one,
        coarse_src_one, coarse_dst_one, parent_two, weight_two, coarse_src_two, coarse_dst_two,
        fine_message_in, fine_message_out, fine_message_gain,
        fine_update_in, fine_update_out, fine_update_gain,
        coarse_message_in, coarse_message_out, coarse_message_gain,
        coarse_update_in, coarse_update_out, coarse_update_gain,
    ) = args

    def whole(shape):
        return pl.BlockSpec(shape, lambda i: (0,) * len(shape))

    def row(v):
        return v.reshape(1, -1)

    steps = EDGES // T1
    base, halo, src4 = pl.pallas_call(
        lambda *refs: halo_kernel(n_gx, n_gy, *refs),
        name="halo",
        grid=(steps,),
        out_shape=(
            jax.ShapeDtypeStruct((EDGES, D), BF16),
            jax.ShapeDtypeStruct((8 * BND, D), BF16),
            jax.ShapeDtypeStruct((EDGES // 128, 128), jnp.int32),
        ),
        in_specs=[
            whole((NF, D)),
            whole((1, BND)),
            whole((EDGES // 128, 128)),
            pl.BlockSpec((1, 1, T1), lambda i: (i, 0, 0)),
            pl.BlockSpec((T1, D), lambda i: (i, 0)),
            whole((3 * D, D)),
        ],
        out_specs=(
            pl.BlockSpec((T1, D), lambda i: (i, 0)),
            whole((8 * BND, D)),
            whole((EDGES // 128, 128)),
        ),
        scratch_shapes=[
            pltpu.VMEM((NF, D), BF16),
            pltpu.VMEM((BND, D), BF16),
            pltpu.VMEM((8, BND, D), BF16),
            pltpu.SemaphoreType.DMA((8,)),
            pltpu.SemaphoreType.DMA((8,)),
        ],
        compiler_params=pltpu.CompilerParams(
            collective_id=0,
            has_side_effects=True,
            vmem_limit_bytes=24 * 2**20,
            dimension_semantics=("arbitrary",),
        ),
    )(
        fine_nodes, row(boundary), fine_src.reshape(-1, 128), fine_dst.reshape(steps, 1, T1),
        edge_latent, fine_message_in,
    )

    steps = EDGES // T2
    fine_new = pl.pallas_call(
        edge_kernel,
        name="edges",
        grid=(steps,),
        out_shape=jax.ShapeDtypeStruct((NF, D), BF16),
        in_specs=[
            whole((NF, D)),
            whole((8 * BND, D)),
            pl.BlockSpec(memory_space=pltpu.SMEM),
            pl.BlockSpec((1, 1, T2), lambda i: (i, 0, 0)),
            pl.BlockSpec((T2, D), lambda i: (i, 0)),
            whole((D, D)),
            whole((D, D)),
            whole((1, D)),
            whole((2 * D, D)),
            whole((D, D)),
            whole((1, D)),
        ],
        out_specs=whole((NF, D)),
        scratch_shapes=[
            pltpu.VMEM((2 * NF * 4, 128), F32),
            pltpu.VMEM((T2 * 4, 128), F32),
            pltpu.VMEM((NF, D), F32),
        ],
        compiler_params=pltpu.CompilerParams(
            vmem_limit_bytes=40 * 2**20,
            dimension_semantics=("arbitrary",),
        ),
    )(
        fine_nodes, halo, src4.reshape(-1), fine_dst.reshape(steps, 1, T2), base,
        fine_message_in, fine_message_out, row(fine_message_gain),
        fine_update_in, fine_update_out, row(fine_update_gain),
    )

    return pl.pallas_call(
        lambda *refs: coarse_kernel(n_gx, n_gy, *refs),
        name="coarse",
        out_shape=jax.ShapeDtypeStruct((NF, D), BF16),
        in_specs=[vmem()] * 15,
        out_specs=vmem(),
        scratch_shapes=[
            pltpu.VMEM((8 * R1, D), BF16),
            pltpu.VMEM((8, R1, D), BF16),
            pltpu.VMEM((N1, D), BF16),
            pltpu.VMEM((8, R1, D), BF16),
            pltpu.VMEM((8 * R2, D), BF16),
            pltpu.VMEM((8, R2, D), BF16),
            pltpu.VMEM((N2, D), BF16),
            pltpu.VMEM((8, R2, D), BF16),
            pltpu.VMEM((N2, D), BF16),
            pltpu.VMEM((8, R2, D), BF16),
            pltpu.VMEM((N1, D), BF16),
            pltpu.VMEM((8, R1, D), BF16),
            pltpu.VMEM((E1, D), F32),
            pltpu.SemaphoreType.DMA((6, 8)),
            pltpu.SemaphoreType.DMA((6, 8)),
        ],
        compiler_params=pltpu.CompilerParams(
            collective_id=1, has_side_effects=True, vmem_limit_bytes=40 * 2**20
        ),
    )(
        fine_new, row(parent_one), row(weight_one), row(coarse_src_one), row(coarse_dst_one),
        row(parent_two), row(weight_two), row(coarse_src_two), row(coarse_dst_two),
        coarse_message_in, coarse_message_out, row(coarse_message_gain),
        coarse_update_in, coarse_update_out, row(coarse_update_gain),
    )


def solution(mesh):
    both = ("gx", "gy")
    in_specs = (P(both, None), P(both, None)) + (P(both),) * 11 + (P(),) * 12
    return jax.shard_map(
        lambda *args: per_device(mesh.shape["gx"], mesh.shape["gy"], args),
        mesh=mesh,
        in_specs=in_specs,
        out_specs=P(both, None),
        check_vma=False,
    )
```

time: 263 us -> 103 us (0.39); the launches traced: 258 us -> 102 us
  Pallas kernels: 0 us -> 93.2 us
  local copies, waits for them, and re-layouts: 82.4 us -> 8.71 us
  matrix products: 64.2 us -> 0 us
  starting transfers between devices: 58.8 us -> 0 us
  waiting for transfers between devices: 33 us -> 0 us
  other arithmetic: 18.9 us -> 0 us
    pallas_call x0 -> x3, Pallas kernels: none -> 93.2 us  [the longest x1 49.1 us: per_device(): pl.pallas_call(lambda *refs: coarse_kernel(n_gx, n_gy, *refs), name='coar...]
    gather x10 -> x0, local copies, waits for them, and re-layouts: 76 us -> none  [the longest x1 28.8 us: per_device(): jnp.take(source_proj, fine_src, axis=0)]
    dot_general x21 -> x0, matrix products: 64.2 us -> none  [the longest x6 30.8 us: finish(): jnp.dot(hidden, project_out, preferred_element_type=jnp.float32)]
    ppermute x28 -> x0, starting transfers between devices: 58.8 us -> none  [the longest x10 39.1 us: padded(): lax.ppermute(head, axis, [((i + 1) % count, i) for i in range(count)])]
    ppermute x28 -> x0, waiting for transfers between devices: 33 us -> none  [the longest x8 19.8 us: passed_along(): return lax.ppermute(value, axis, pairs)]
    reduce_sum x6 -> x0, other arithmetic: 7.41 us -> none  [normed(): spread = jnp.mean(centred * centred, axis=-1, keepdims=True)]
    unnamed x85 -> x57, local copies, waits for them, and re-layouts: 4.93 us -> 8.66 us
    convert_element_type x9 -> x0, other arithmetic: 3.63 us -> none  [the longest x1 1.65 us: per_device(): (fine_new.astype(jnp.float32) + lift_rows(level_one_final, CB1, parent_on...]
  transfers between devices with their start and end apart: 28 -> 0, of which waited for: 19 -> 0; matrix products, arithmetic and copies ran while one was open for 18% -> 0% of each run, Pallas kernels for 0% -> 0%
where the time goes in v1:
time: 103 us; the launch traced here: 102 us
  Pallas kernels  93.2 us (90%)
  local copies, waits for them, and re-layouts  8.71 us (8%)
    pallas_call x1, Pallas kernels, per_device(): pl.pallas_call(lambda *refs: coarse_kernel(n_gx, n_gy, *refs), name='coar...  49.1 us
    pallas_call x1, Pallas kernels, per_device(): pl.pallas_call(lambda *refs: halo_kernel(n_gx, n_gy, *refs), name='halo',...  22.5 us
    pallas_call x1, Pallas kernels, per_device(): pl.pallas_call(edge_kernel, name='edges', grid=(steps,), out_shape=jax.Sh...  21.6 us
    unnamed x57, local copies, waits for them, and re-layouts  8.66 us

profile of v1, /device:TPU:1, one launch (start us, length us, event | category | flops | bytes accessed | tf_op | source)
XLA Modules:
  0.0 102.3 jit_solution(5986230378173912)
XLA Ops:
  0.0 1.4 %copy-done = bf16[1536,512]{1,0:T(8,128)(2,1)S(1)} copy-done((bf16[1536,512]{1,0:T(8,128)(2,1)S(1)}, bf16[1536,512]{1,0:T(8,128)(2,1)}, u32[]{:S(2)}) %copy-start) | copy-done | bytes 1572888
  1.4 2.8 %copy-done.2 = bf16[6144,512]{1,0:T(8,128)(2,1)S(1)} copy-done((bf16[6144,512]{1,0:T(8,128)(2,1)S(1)}, bf16[6144,512]{1,0:T(8,128)(2,1)}, u32[]{:S(2)}) %copy-start.2) | copy-done | bytes 6291480
  4.2 1.2 %copy-done.3 = bf16[1024,512]{1,0:T(8,128)(2,1)S(1)} copy-done((bf16[1024,512]{1,0:T(8,128)(2,1)S(1)}, bf16[1024,512]{1,0:T(8,128)(2,1)}, u32[]{:S(2)}) %copy-start.3) | copy-done | bytes 1048600
  5.5 0.7 copy-done.12
  6.2 0.7 copy-done.14
  6.9 0.7 copy-done.17
  7.6 22.5 %halo.1 = (bf16[6144,512]{1,0:T(8,128)(2,1)S(1)}, bf16[1024,512]{1,0:T(8,128)(2,1)S(1)}, s32[48,128]{1,0:T(8,128)S(1)}) custom-call(bf16[1024,512]{1,0:T(8,128)(2,1)S(1)} %copy-done.3, s32[1,128]{1,0:T(1,128)S(1)} %bitcast.12, s32[48,128]{1,0:T(8,128)S(1)} %bitcast.8, s32[12,1,512]{2,1,0:T(1,128)S(1)} %bitcast.6, bf16[6144,512]{1,0:T(8,128)(2,1)S(1)} %copy-done.2, ...), custom_call_target="tpu_custom_call" | custom-call | tf_op jit(solution)/shard_map/halo/pallas_call | solution.py:306
  30.2 0.0 copy-start.18
  30.2 0.0 copy-start.19
  30.2 0.0 copy-start.20
  30.2 0.0 copy-start.25
  30.2 0.0 copy-start.26
  30.3 0.0 copy-start.21
  30.3 0.0 copy-start.22
  30.3 0.0 copy-start.27
  30.3 0.0 copy-start.6
  30.3 0.0 copy-start.7
  30.3 0.0 copy-start.10
  30.3 0.0 copy-start.11
  30.3 0.0 copy-start.15
  30.3 0.0 copy-start.16
  30.4 21.6 %edges.1.refs_0_ = bf16[1024,512]{1,0:T(8,128)(2,1)S(1)} custom-call(bf16[1024,512]{1,0:T(8,128)(2,1)S(1)} %copy-done.4, bf16[1024,512]{1,0:T(8,128)(2,1)S(1)} %get-tuple-element.8.halo, s32[6144]{0:T(1024)S(1)} %bitcast.9, s32[12,1,512]{2,1,0:T(1,128)S(1)} %bitcast.7, bf16[6144,512]{1,0:T(8,128)(2,1)S(1)} %get-tuple-element.10.base, ...), custom_call_target="tpu_custom_call" | custom-call | tf_op jit(solution)/shard_map/edges/pallas_call | solution.py:347
  52.2 49.1 %coarse.1 = bf16[1024,512]{1,0:T(8,128)(2,1)S(1)} custom-call(bf16[1024,512]{1,0:T(8,128)(2,1)S(1)} %edges.1.refs_0_, s32[1,1024]{1,0:T(1,128)S(1)} %bitcast.10, bf16[1,1024]{1,0:T(2,128)(2,1)S(1)} %reshape.56.refs_2_, s32[1,1536]{1,0:T(1,128)S(1)} %reshape.57.refs_3_, s32[1,1536]{1,0:T(1,128)S(1)} %reshape.58.refs_4_, s32[1,256]{1,0:T(1,128)S(1)} %bitcast.11, ...), custom_call_target="tpu_custom_call" | custom-call | tf_op jit(solution)/shard_map/coarse/pallas_call | solution.py:381
  101.3 1.0 copy.27
  (46 shorter events, 0.1 us)
Async XLA Ops:
  0.0 30.1 %copy-start.23 = (bf16[512]{0:T(512)(128)(2,1)S(1)}, bf16[512]{0:T(512)(128)(2,1)}, u32[]{:S(2)}) copy-start(bf16[512]{0:T(512)(128)(2,1)} %param.40) | copy-start | bytes 3076
  0.0 30.1 %copy-start.24 = (bf16[512]{0:T(512)(128)(2,1)S(1)}, bf16[512]{0:T(512)(128)(2,1)}, u32[]{:S(2)}) copy-start(bf16[512]{0:T(512)(128)(2,1)} %param.43) | copy-start | bytes 3076
  0.0 1.4 %copy-start = (bf16[1536,512]{1,0:T(8,128)(2,1)S(1)}, bf16[1536,512]{1,0:T(8,128)(2,1)}, u32[]{:S(2)}) copy-start(bf16[1536,512]{1,0:T(8,128)(2,1)} %w_src.1) | copy-start | bytes 4718596
  1.4 2.8 %copy-start.2 = (bf16[6144,512]{1,0:T(8,128)(2,1)S(1)}, bf16[6144,512]{1,0:T(8,128)(2,1)}, u32[]{:S(2)}) copy-start(bf16[6144,512]{1,0:T(8,128)(2,1)} %refs_4_.1) | copy-start | bytes 18874372
  7.6 22.6 %copy-start.1 = (bf16[1536,512]{1,0:T(8,128)(2,1)S(1)}, bf16[1536,512]{1,0:T(8,128)(2,1)}, u32[]{:S(2)}) copy-start(bf16[1536,512]{1,0:T(8,128)(2,1)} %w_src.1) | copy-start | bytes 4718596
  7.6 22.6 %copy-start.4 = (bf16[1024,512]{1,0:T(8,128)(2,1)S(1)}, bf16[1024,512]{1,0:T(8,128)(2,1)}, u32[]{:S(2)}) copy-start(bf16[1024,512]{1,0:T(8,128)(2,1)} %nodes.1) | copy-start | bytes 3145732
  7.6 22.6 %copy-start.5 = (bf16[1024,512]{1,0:T(8,128)(2,1)S(1)}, bf16[1024,512]{1,0:T(8,128)(2,1)}, u32[]{:S(2)}) copy-start(bf16[1024,512]{1,0:T(8,128)(2,1)} %up_in.1) | copy-start | bytes 3145732
  7.6 22.6 %copy-start.8 = (bf16[512,512]{1,0:T(8,128)(2,1)S(1)}, bf16[512,512]{1,0:T(8,128)(2,1)}, u32[]{:S(2)}) copy-start(bf16[512,512]{1,0:T(8,128)(2,1)} %w_out.1) | copy-start | bytes 1572868
  7.6 22.6 %copy-start.9 = (bf16[512,512]{1,0:T(8,128)(2,1)S(1)}, bf16[512,512]{1,0:T(8,128)(2,1)}, u32[]{:S(2)}) copy-start(bf16[512,512]{1,0:T(8,128)(2,1)} %up_out.1) | copy-start | bytes 1572868
  7.6 22.6 %copy-start.13 = (s32[6144]{0:T(1024)S(1)}, s32[6144]{0:T(1024)}, u32[]{:S(2)}) copy-start(s32[6144]{0:T(1024)} %param.29) | copy-start | bytes 73732
  30.2 21.8 %copy-start.18 = (s32[1536]{0:T(1024)S(1)}, s32[1536]{0:T(1024)}, u32[]{:S(2)}) copy-start(s32[1536]{0:T(1024)} %param.32) | copy-start | bytes 18436
  30.2 21.8 %copy-start.19 = (s32[1536]{0:T(1024)S(1)}, s32[1536]{0:T(1024)}, u32[]{:S(2)}) copy-start(s32[1536]{0:T(1024)} %param.33) | copy-start | bytes 18436
  30.2 21.8 %copy-start.20 = (bf16[1024]{0:T(1024)(128)(2,1)S(1)}, bf16[1024]{0:T(1024)(128)(2,1)}, u32[]{:S(2)}) copy-start(bf16[1024]{0:T(1024)(128)(2,1)} %param.31) | copy-start | bytes 6148
  30.2 21.8 %copy-start.25 = (bf16[512]{0:T(512)(128)(2,1)S(1)}, bf16[512]{0:T(512)(128)(2,1)}, u32[]{:S(2)}) copy-start(bf16[512]{0:T(512)(128)(2,1)} %param.46) | copy-start | bytes 3076
  30.2 21.8 %copy-start.26 = (bf16[512]{0:T(512)(128)(2,1)S(1)}, bf16[512]{0:T(512)(128)(2,1)}, u32[]{:S(2)}) copy-start(bf16[512]{0:T(512)(128)(2,1)} %param.49) | copy-start | bytes 3076
  30.3 21.8 %copy-start.21 = (s32[384]{0:T(512)S(1)}, s32[384]{0:T(512)}, u32[]{:S(2)}) copy-start(s32[384]{0:T(512)} %param.36) | copy-start | bytes 4612
  30.3 21.8 %copy-start.22 = (s32[384]{0:T(512)S(1)}, s32[384]{0:T(512)}, u32[]{:S(2)}) copy-start(s32[384]{0:T(512)} %param.37) | copy-start | bytes 4612
  30.3 21.8 %copy-start.27 = (bf16[256]{0:T(256)(128)(2,1)S(1)}, bf16[256]{0:T(256)(128)(2,1)}, u32[]{:S(2)}) copy-start(bf16[256]{0:T(256)(128)(2,1)} %param.35) | copy-start | bytes 1540
  30.3 21.8 %copy-start.6 = (bf16[1024,512]{1,0:T(8,128)(2,1)S(1)}, bf16[1024,512]{1,0:T(8,128)(2,1)}, u32[]{:S(2)}) copy-start(bf16[1024,512]{1,0:T(8,128)(2,1)} %refs_9_.1) | copy-start | bytes 3145732
  30.3 21.8 %copy-start.7 = (bf16[1024,512]{1,0:T(8,128)(2,1)S(1)}, bf16[1024,512]{1,0:T(8,128)(2,1)}, u32[]{:S(2)}) copy-start(bf16[1024,512]{1,0:T(8,128)(2,1)} %refs_12_.1) | copy-start | bytes 3145732
  30.3 21.8 %copy-start.10 = (bf16[512,512]{1,0:T(8,128)(2,1)S(1)}, bf16[512,512]{1,0:T(8,128)(2,1)}, u32[]{:S(2)}) copy-start(bf16[512,512]{1,0:T(8,128)(2,1)} %refs_10_.1) | copy-start | bytes 1572868
  30.3 21.8 %copy-start.11 = (bf16[512,512]{1,0:T(8,128)(2,1)S(1)}, bf16[512,512]{1,0:T(8,128)(2,1)}, u32[]{:S(2)}) copy-start(bf16[512,512]{1,0:T(8,128)(2,1)} %refs_13_.1) | copy-start | bytes 1572868
  30.3 21.8 %copy-start.15 = (s32[1024]{0:T(1024)S(1)}, s32[1024]{0:T(1024)}, u32[]{:S(2)}) copy-start(s32[1024]{0:T(1024)} %param.30) | copy-start | bytes 12292
  30.3 21.8 %copy-start.16 = (s32[256]{0:T(256)S(1)}, s32[256]{0:T(256)}, u32[]{:S(2)}) copy-start(s32[256]{0:T(256)} %param.34) | copy-start | bytes 3076
  (4 other events, 3.4 us)

commit v2 on v1

v2 whole, which is shorter than its diff:
```python
import jax
import jax.numpy as jnp
from jax import lax
from jax.experimental import pallas as pl
from jax.experimental.pallas import tpu as pltpu
from jax.sharding import PartitionSpec as P

MESH = pl.DeviceIdType.MESH
BF16 = jnp.bfloat16
F32 = jnp.float32

D = 512
NF = 1024
BND = 128
EDGES = 6144
N1, R1, E1 = 256, 64, 1536
N2, R2, E2 = 64, 32, 384
T1 = 512
T2 = 512
OFFSETS = [(k // 3 - 1, k % 3 - 1) for k in range(9) if k != 4]


def neighbours(n_gx, n_gy):
    ix, iy = lax.axis_index("gx"), lax.axis_index("gy")
    return [
        (lax.rem(ix + dx + n_gx, n_gx), lax.rem(iy + dy + n_gy, n_gy)) for dx, dy in OFFSETS
    ]


def greet(around):
    barrier = pltpu.get_barrier_semaphore()
    for who in around:
        pl.semaphore_signal(barrier, inc=1, device_id=who, device_id_type=MESH)


def all_greeted():
    pl.semaphore_wait(pltpu.get_barrier_semaphore(), 8)


def exchange(around, piece, landing, send_sem, recv_sem):
    copies = []
    for s, who in enumerate(around):
        copies.append(
            pltpu.make_async_remote_copy(
                src_ref=piece(s),
                dst_ref=landing.at[7 - s],
                send_sem=send_sem.at[s],
                recv_sem=recv_sem.at[7 - s],
                device_id=who,
                device_id_type=MESH,
            )
        )
    for copy in copies:
        copy.start()
    return copies


def finished(copies):
    for copy in copies:
        copy.wait()


def dot(a, b):
    return jnp.dot(a, b, preferred_element_type=F32)


def silu(v):
    half = 0.5 * v
    return half + half * jnp.tanh(half)


def normed(v, gain):
    centred = v - jnp.mean(v, axis=-1, keepdims=True)
    spread = jnp.mean(centred * centred, axis=-1, keepdims=True)
    return centred * lax.rsqrt(spread + 1e-05) * gain


def packed_numbers(numbers, local, rim):
    return jnp.where(numbers >= local + 5 * rim, numbers - rim, numbers)


def pick_rows(row, width, first=0):
    across = jnp.broadcast_to(row - first, (128, 128)).T
    lane = lax.broadcasted_iota(jnp.int32, (128, 128), 1)
    return jnp.concatenate(
        [
            jnp.where(across == lane + 128 * c, 1.0, 0.0).astype(BF16)
            for c in range(width // 128)
        ],
        axis=1,
    )


def pick_matrix(rows, start, count, width, first=0):
    return jnp.concatenate(
        [pick_rows(rows[:, start + j : start + j + 128], width, first) for j in range(0, count, 128)],
        axis=0,
    )


def gather_sums(rows, height):
    down = lax.broadcasted_iota(jnp.int32, (height, rows.shape[1]), 0)
    return jnp.where(down == rows, 1.0, 0.0).astype(BF16)


def spread_sums(states, parents, weights, local, rim):
    numbers = packed_numbers(parents, local, rim)
    down = lax.broadcasted_iota(jnp.int32, (local + 8 * rim, parents.shape[1]), 0)
    spread = jnp.where(down == numbers, weights, 0.0).astype(BF16)
    return dot(spread, states)


def node_update(states, incoming, up_in, up_out, up_gain):
    update = silu(dot(states, up_in[:D]) + dot(incoming, up_in[D:])).astype(BF16)
    return (
        states.astype(F32) + normed(dot(update, up_out[...]), flat_row(up_gain))
    ).astype(BF16)


def coarse_part(
    around, fine, parent1, weight1, src1, dst1, parent2, weight2, src2, dst2,
    msg_in, msg_out, msg_gain, up_in, up_out, up_gain, out,
    sums1, land_a, level1, land_b, sums2, land_c, level2, land_d, new2, land_e, final1, land_f,
    preact, send_sem, recv_sem,
):
    def swap(i, piece, landing):
        return exchange(around, piece, landing, send_sem.at[i], recv_sem.at[i])

    parents = packed_numbers(parent1[...], N1, R1)
    spread = spread_sums(fine[...], parent1[...], flat_row(weight1), N1, R1)
    sums1[...] = spread[N1:].astype(BF16)
    moving = swap(0, lambda s: sums1.at[pl.ds(s * R1, R1)], land_a)
    down_rows = gather_sums(dst1[...], N1)
    finished(moving)
    rim = spread[:R1]
    for s in range(8):
        rim = rim + land_a[s].astype(F32)
    level1[...] = jnp.concatenate([rim, spread[R1:N1]], axis=0).astype(BF16)

    moving = swap(1, lambda s: level1.at[pl.ds(0, R1)], land_b)
    own = dot(level1[...], msg_in[:D]).astype(BF16)
    mine = dot(level1[...], msg_in[D:]).astype(BF16)
    numbers = packed_numbers(src1[...], N1, R1)
    for t in range(0, E1, 512):
        preact[pl.ds(t, 512), :] = dot(pick_matrix(numbers, t, 512, N1), own) + dot(
            pick_matrix(dst1, t, 512, N1), mine
        )
    finished(moving)
    beyond = dot(land_b[...].reshape(8 * R1, D), msg_in[:D]).astype(BF16)
    incoming = jnp.zeros((N1, D), F32)
    for t in range(0, E1, 512):
        hidden = silu(
            preact[pl.ds(t, 512), :] + dot(pick_matrix(numbers, t, 512, 8 * R1, N1), beyond)
        ).astype(BF16)
        messages = normed(dot(hidden, msg_out[...]), flat_row(msg_gain)).astype(BF16)
        incoming = incoming + dot(down_rows[:, t : t + 512], messages)
    new1 = node_update(level1[...], incoming.astype(BF16), up_in, up_out, up_gain)

    spread = spread_sums(new1, parent2[...], flat_row(weight2), N2, R2)
    sums2[...] = spread[N2:].astype(BF16)
    moving = swap(2, lambda s: sums2.at[pl.ds(s * R2, R2)], land_c)
    finished(moving)
    rim = spread[:R2]
    for s in range(8):
        rim = rim + land_c[s].astype(F32)
    level2[...] = jnp.concatenate([rim, spread[R2:N2]], axis=0).astype(BF16)

    moving = swap(3, lambda s: level2.at[pl.ds(0, R2)], land_d)
    mine = dot(level2[...], msg_in[D:]).astype(BF16)
    own = dot(level2[...], msg_in[:D]).astype(BF16)
    numbers = packed_numbers(src2[...], N2, R2)
    pad = jnp.zeros((64, D), BF16)
    start = dot(pick_matrix(dst2, 0, E2, 128), jnp.concatenate([mine, pad], axis=0)) + dot(
        pick_matrix(numbers, 0, E2, 128), jnp.concatenate([own, pad], axis=0)
    )
    finished(moving)
    beyond = dot(land_d[...].reshape(8 * R2, D), msg_in[:D]).astype(BF16)
    hidden = silu(start + dot(pick_matrix(numbers, 0, E2, 8 * R2, N2), beyond)).astype(BF16)
    messages = normed(dot(hidden, msg_out[...]), flat_row(msg_gain)).astype(BF16)
    incoming = dot(gather_sums(dst2[...], N2), messages).astype(BF16)
    new2[...] = node_update(level2[...], incoming, up_in, up_out, up_gain)

    moving = swap(4, lambda s: new2.at[pl.ds(0, R2)], land_e)
    numbers = packed_numbers(parent2[...], N2, R2)
    lift = new1.astype(F32) + dot(
        pick_matrix(numbers, 0, N1, 128), jnp.concatenate([new2[...], pad], axis=0)
    )
    finished(moving)
    final1[...] = (
        lift + dot(pick_matrix(numbers, 0, N1, 8 * R2, N2), land_e[...].reshape(8 * R2, D))
    ).astype(BF16)

    moving = swap(5, lambda s: final1.at[pl.ds(0, R1)], land_f)
    for t in range(0, NF, 512):
        preact[pl.ds(t, 512), :] = fine[pl.ds(t, 512), :].astype(F32) + dot(
            pick_matrix(parents, t, 512, N1), final1[...]
        )
    finished(moving)
    rims = land_f[...].reshape(8 * R1, D)
    for t in range(0, NF, 512):
        out[pl.ds(t, 512), :] = (
            preact[pl.ds(t, 512), :] + dot(pick_matrix(parents, t, 512, 8 * R1, N1), rims)
        ).astype(BF16)


LOADS = (
    "nodes", "bnd", "w_in", "dst", "src", "w_out", "gain", "up_in", "up_out", "up_gain",
    "parent1", "weight1", "src1", "dst1", "parent2", "weight2", "src2", "dst2",
    "msg_in", "msg_out", "msg_gain", "cup_in", "cup_out", "cup_gain",
)


def flat_row(ref):
    return ref[...].astype(F32).reshape(1, -1)


def block_kernel(n_gx, n_gy, *refs):
    count = len(LOADS)
    far = dict(zip(LOADS, refs[:count]))
    latent_far, out = refs[count], refs[count + 1]
    here = dict(zip(LOADS, refs[count + 2 : 2 * count + 2]))
    (
        latent, table, picked, total, target, edge_rows, halo,
        fine, sums1, land_a, level1, land_b, sums2, land_c, level2, land_d, new2, land_e,
        final1, land_f, preact, load_sem, latent_sem, halo_send, halo_recv,
        send_sem, recv_sem,
    ) = refs[2 * count + 2 :]
    around = neighbours(n_gx, n_gy)
    greet(around)
    loads = {
        name: pltpu.make_async_copy(far[name], here[name], load_sem.at[i])
        for i, name in enumerate(LOADS)
    }

    def latent_copy(i):
        part = pl.ds(pl.multiple_of(i * T1, T1), T1)
        return pltpu.make_async_copy(latent_far.at[part], latent.at[part], latent_sem.at[i])

    for name in ("nodes", "bnd", "w_in", "dst", "src"):
        loads[name].start()
    for i in range(EDGES // T1):
        latent_copy(i).start()
    for name in LOADS[5:]:
        loads[name].start()

    nodes, dst, w_in = here["nodes"], here["dst"], here["w_in"]
    for name in ("nodes", "bnd"):
        loads[name].wait()
    edge_rows[...] = dot(pick_rows(here["bnd"][...], NF), nodes[...]).astype(BF16)
    all_greeted()
    halo_moving = exchange(around, lambda s: edge_rows, halo, halo_send, halo_recv)

    for name in ("w_in", "dst", "src"):
        loads[name].wait()
    target[...] = dot(nodes[...], w_in[D : 2 * D]).astype(BF16)

    def base_step(i, _):
        latent_copy(i).wait()
        part = pl.ds(pl.multiple_of(i * T1, T1), T1)
        latent[part, :] = (
            dot(pick_matrix(dst[i], 0, T1, NF), target[...]) + dot(latent[part, :], w_in[2 * D :])
        ).astype(BF16)
        return 0

    lax.fori_loop(0, EDGES // T1, base_step, 0)

    def fill(rows, start):
        value = dot(rows, w_in[:D])
        table[pl.ds(start, 256)] = value.reshape(256, 4, 128)

    for c in range(0, NF, 256):
        fill(nodes[pl.ds(c, 256), :], c)
    total[...] = jnp.zeros_like(total)
    for name in LOADS[5:]:
        loads[name].wait()
    finished(halo_moving)
    for s in range(0, 8, 2):
        fill(halo[pl.ds(s, 2)].reshape(2 * BND, D), NF + BND * (s + s // 4))

    def pick(first):
        for e in range(T2):
            picked[pl.ds(4 * e, 4), :] = table[here["src"][first + e]]

    pick(0)

    def edge_step(i, _):
        source = jnp.concatenate(
            [picked[pl.ds(j, T2, stride=4), :] for j in range(4)], axis=1
        )
        part = pl.ds(pl.multiple_of(i * T2, T2), T2)
        hidden = silu(source + latent[part, :].astype(F32)).astype(BF16)
        pick(jnp.minimum(i + 1, EDGES // T2 - 1) * T2)
        messages = normed(dot(hidden, here["w_out"][...]), flat_row(here["gain"])).astype(BF16)
        total[...] += dot(gather_sums(dst[i], NF), messages)
        return 0

    lax.fori_loop(0, EDGES // T2, edge_step, 0)
    fine[...] = node_update(
        nodes[...], total[...].astype(BF16), here["up_in"], here["up_out"], here["up_gain"]
    )

    coarse_part(
        around, fine, *[here[name] for name in LOADS[10:]], out,
        sums1, land_a, level1, land_b, sums2, land_c, level2, land_d, new2, land_e,
        final1, land_f, preact, send_sem, recv_sem,
    )


def per_device(n_gx, n_gy, args):
    (
        fine_nodes, edge_latent, boundary, fine_src, fine_dst, parent_one, weight_one,
        coarse_src_one, coarse_dst_one, parent_two, weight_two, coarse_src_two, coarse_dst_two,
        fine_message_in, fine_message_out, fine_message_gain,
        fine_update_in, fine_update_out, fine_update_gain,
        coarse_message_in, coarse_message_out, coarse_message_gain,
        coarse_update_in, coarse_update_out, coarse_update_gain,
    ) = args

    def row(v):
        return v.reshape(1, -1)

    given = dict(
        nodes=fine_nodes, bnd=row(boundary), w_in=fine_message_in,
        dst=fine_dst.reshape(EDGES // T1, 1, T1), src=fine_src,
        w_out=fine_message_out, gain=fine_message_gain,
        up_in=fine_update_in, up_out=fine_update_out, up_gain=fine_update_gain,
        parent1=row(parent_one), weight1=weight_one,
        src1=row(coarse_src_one), dst1=row(coarse_dst_one),
        parent2=row(parent_two), weight2=weight_two,
        src2=row(coarse_src_two), dst2=row(coarse_dst_two),
        msg_in=coarse_message_in, msg_out=coarse_message_out, msg_gain=coarse_message_gain,
        cup_in=coarse_update_in, cup_out=coarse_update_out, cup_gain=coarse_update_gain,
    )
    operands = [given[name] for name in LOADS]
    return pl.pallas_call(
        lambda *refs: block_kernel(n_gx, n_gy, *refs),
        name="block",
        out_shape=jax.ShapeDtypeStruct((NF, D), BF16),
        in_specs=[pl.BlockSpec(memory_space=pltpu.HBM)] * (len(LOADS) + 1),
        out_specs=pl.BlockSpec(memory_space=pltpu.VMEM),
        scratch_shapes=[
            (pltpu.SMEM if name == "src" else pltpu.VMEM)(v.shape, v.dtype)
            for name, v in zip(LOADS, operands)
        ]
        + [
            pltpu.VMEM((EDGES, D), BF16),
            pltpu.VMEM((NF + 9 * BND, 4, 128), F32),
            pltpu.VMEM((T2 * 4, 128), F32),
            pltpu.VMEM((NF, D), F32),
            pltpu.VMEM((NF, D), BF16),
            pltpu.VMEM((BND, D), BF16),
            pltpu.VMEM((8, BND, D), BF16),
            pltpu.VMEM((NF, D), BF16),
            pltpu.VMEM((8 * R1, D), BF16),
            pltpu.VMEM((8, R1, D), BF16),
            pltpu.VMEM((N1, D), BF16),
            pltpu.VMEM((8, R1, D), BF16),
            pltpu.VMEM((8 * R2, D), BF16),
            pltpu.VMEM((8, R2, D), BF16),
            pltpu.VMEM((N2, D), BF16),
            pltpu.VMEM((8, R2, D), BF16),
            pltpu.VMEM((N2, D), BF16),
            pltpu.VMEM((8, R2, D), BF16),
            pltpu.VMEM((N1, D), BF16),
            pltpu.VMEM((8, R1, D), BF16),
            pltpu.VMEM((E1, D), F32),
            pltpu.SemaphoreType.DMA((len(LOADS),)),
            pltpu.SemaphoreType.DMA((EDGES // T1,)),
            pltpu.SemaphoreType.DMA((8,)),
            pltpu.SemaphoreType.DMA((8,)),
            pltpu.SemaphoreType.DMA((6, 8)),
            pltpu.SemaphoreType.DMA((6, 8)),
        ],
        compiler_params=pltpu.CompilerParams(
            collective_id=0, has_side_effects=True, vmem_limit_bytes=58 * 2**20
        ),
    )(*operands, edge_latent)


def solution(mesh):
    both = ("gx", "gy")
    in_specs = (P(both, None), P(both, None)) + (P(both),) * 11 + (P(),) * 12
    return jax.shard_map(
        lambda *args: per_device(mesh.shape["gx"], mesh.shape["gy"], args),
        mesh=mesh,
        in_specs=in_specs,
        out_specs=P(both, None),
        check_vma=False,
    )
```

time: 103 us -> 99.6 us (0.967)
  local copies, waits for them, and re-layouts: 8.71 us -> 7.36 us
  Pallas kernels: 93.2 us -> 92 us
    unnamed x57 -> x1, local copies, waits for them, and re-layouts: 8.66 us -> 2.26 us
    reshape x10 -> x4, local copies, waits for them, and re-layouts: 0.05 us -> 5.1 us  [row(): return v.reshape(1, -1)]
    pallas_call x3 -> x1, Pallas kernels: 93.2 us -> 92 us  [per_device(): pl.pallas_call(lambda *refs: block_kernel(n_gx, n_gy, *refs), name='block...]
where the time goes in v2:
time: 99.6 us; the launch traced here: 99.4 us
  Pallas kernels  92 us (92%)
  local copies, waits for them, and re-layouts  7.36 us (7%)
    pallas_call x1, Pallas kernels, per_device(): pl.pallas_call(lambda *refs: block_kernel(n_gx, n_gy, *refs), name='block...  92 us
    reshape x4, local copies, waits for them, and re-layouts, row(): return v.reshape(1, -1)  5.1 us
    unnamed x1, local copies, waits for them, and re-layouts  2.26 us

profile of v2, /device:TPU:1, one launch (start us, length us, event | category | flops | bytes accessed | tf_op | source)
XLA Modules:
  0.0 99.4 jit_solution(14360939536012893258)
XLA Ops:
  0.0 1.3 %reshape.30.refs_16_ = s32[1,384]{1,0:T(1,128)} reshape(s32[384]{0:T(512)} %param.36) | data formatting | bytes 3072 | tf_op jit(solution)/shard_map/reshape | solution.py:320
  1.3 1.2 %reshape.31.refs_17_ = s32[1,384]{1,0:T(1,128)} reshape(s32[384]{0:T(512)} %param.37) | data formatting | bytes 3072 | tf_op jit(solution)/shard_map/reshape | solution.py:320
  2.5 1.3 %reshape.27.refs_12_ = s32[1,1536]{1,0:T(1,128)} reshape(s32[1536]{0:T(1024)} %param.32) | data formatting | bytes 12288 | tf_op jit(solution)/shard_map/reshape | solution.py:320
  3.8 1.3 %reshape.28.refs_13_ = s32[1,1536]{1,0:T(1,128)} reshape(s32[1536]{0:T(1024)} %param.33) | data formatting | bytes 12288 | tf_op jit(solution)/shard_map/reshape | solution.py:320
  5.1 92.0 %block.1 = bf16[1024,512]{1,0:T(8,128)(2,1)} custom-call(bf16[1024,512]{1,0:T(8,128)(2,1)} %refs_0_.1, s32[1,128]{1,0:T(1,128)} %bitcast.7, bf16[1536,512]{1,0:T(8,128)(2,1)} %refs_2_.1, s32[12,1,512]{2,1,0:T(1,128)} %bitcast.4, s32[6144]{0:T(1024)} %refs_4_.1, bf16[512,512]{1,0:T(8,128)(2,1)} %refs_5_.1, bf16[512]{0:T(512)(128)(2,1)} %refs_6_.1, ...), custom_call_target="tpu_custom_call" | custom-call | tf_op jit(solution)/shard_map/block/pallas_call | solution.py:335
  97.1 2.3 %copy.27 = bf16[1024,512]{1,0:T(8,128)(2,1)} copy(bf16[1024,512]{1,0:T(8,128)(2,1)} %block.1) | data formatting | bytes 2097152

commit v3 on v2

--- a/solution.py
+++ b/solution.py
@@ -16,7 +16,8 @@
 N1, R1, E1 = 256, 64, 1536
 N2, R2, E2 = 64, 32, 384
 T1 = 512
-T2 = 512
+T2 = 1024
+EARLY = 4
 OFFSETS = [(k // 3 - 1, k % 3 - 1) for k in range(9) if k != 4]
 
 
@@ -69,10 +70,11 @@
     return half + half * jnp.tanh(half)
 
 
-def normed(v, gain):
+def normed(v, gain=None):
     centred = v - jnp.mean(v, axis=-1, keepdims=True)
     spread = jnp.mean(centred * centred, axis=-1, keepdims=True)
-    return centred * lax.rsqrt(spread + 1e-05) * gain
+    scaled = centred * lax.rsqrt(spread + 1e-05)
+    return scaled if gain is None else scaled * gain
 
 
 def packed_numbers(numbers, local, rim):
@@ -126,11 +128,12 @@
     def swap(i, piece, landing):
         return exchange(around, piece, landing, send_sem.at[i], recv_sem.at[i])
 
+    src1, dst1, src2, dst2 = (ref[...].reshape(1, -1) for ref in (src1, dst1, src2, dst2))
     parents = packed_numbers(parent1[...], N1, R1)
     spread = spread_sums(fine[...], parent1[...], flat_row(weight1), N1, R1)
     sums1[...] = spread[N1:].astype(BF16)
     moving = swap(0, lambda s: sums1.at[pl.ds(s * R1, R1)], land_a)
-    down_rows = gather_sums(dst1[...], N1)
+    down_rows = gather_sums(dst1, N1)
     finished(moving)
     rim = spread[:R1]
     for s in range(8):
@@ -140,7 +143,7 @@
     moving = swap(1, lambda s: level1.at[pl.ds(0, R1)], land_b)
     own = dot(level1[...], msg_in[:D]).astype(BF16)
     mine = dot(level1[...], msg_in[D:]).astype(BF16)
-    numbers = packed_numbers(src1[...], N1, R1)
+    numbers = packed_numbers(src1, N1, R1)
     for t in range(0, E1, 512):
         preact[pl.ds(t, 512), :] = dot(pick_matrix(numbers, t, 512, N1), own) + dot(
             pick_matrix(dst1, t, 512, N1), mine
@@ -168,7 +171,7 @@
     moving = swap(3, lambda s: level2.at[pl.ds(0, R2)], land_d)
     mine = dot(level2[...], msg_in[D:]).astype(BF16)
     own = dot(level2[...], msg_in[:D]).astype(BF16)
-    numbers = packed_numbers(src2[...], N2, R2)
+    numbers = packed_numbers(src2, N2, R2)
     pad = jnp.zeros((64, D), BF16)
     start = dot(pick_matrix(dst2, 0, E2, 128), jnp.concatenate([mine, pad], axis=0)) + dot(
         pick_matrix(numbers, 0, E2, 128), jnp.concatenate([own, pad], axis=0)
@@ -177,7 +180,7 @@
     beyond = dot(land_d[...].reshape(8 * R2, D), msg_in[:D]).astype(BF16)
     hidden = silu(start + dot(pick_matrix(numbers, 0, E2, 8 * R2, N2), beyond)).astype(BF16)
     messages = normed(dot(hidden, msg_out[...]), flat_row(msg_gain)).astype(BF16)
-    incoming = dot(gather_sums(dst2[...], N2), messages).astype(BF16)
+    incoming = dot(gather_sums(dst2, N2), messages).astype(BF16)
     new2[...] = node_update(level2[...], incoming, up_in, up_out, up_gain)
 
     moving = swap(4, lambda s: new2.at[pl.ds(0, R2)], land_e)
@@ -220,7 +223,7 @@
     latent_far, out = refs[count], refs[count + 1]
     here = dict(zip(LOADS, refs[count + 2 : 2 * count + 2]))
     (
-        latent, table, picked, total, target, edge_rows, halo,
+        latent, base, table, picked, picked_b, messages_a, messages_b, total, target, edge_rows, halo,
         fine, sums1, land_a, level1, land_b, sums2, land_c, level2, land_d, new2, land_e,
         final1, land_f, preact, load_sem, latent_sem, halo_send, halo_recv,
         send_sem, recv_sem,
@@ -247,25 +250,25 @@
     for name in ("nodes", "bnd"):
         loads[name].wait()
     edge_rows[...] = dot(pick_rows(here["bnd"][...], NF), nodes[...]).astype(BF16)
-    all_greeted()
-    halo_moving = exchange(around, lambda s: edge_rows, halo, halo_send, halo_recv)
-
     for name in ("w_in", "dst", "src"):
         loads[name].wait()
-    target[...] = dot(nodes[...], w_in[D : 2 * D]).astype(BF16)
+    target[...] = (0.5 * dot(nodes[...], w_in[D : 2 * D])).astype(BF16)
 
     def base_step(i, _):
         latent_copy(i).wait()
         part = pl.ds(pl.multiple_of(i * T1, T1), T1)
-        latent[part, :] = (
-            dot(pick_matrix(dst[i], 0, T1, NF), target[...]) + dot(latent[part, :], w_in[2 * D :])
-        ).astype(BF16)
+        base[part, :] = dot(pick_matrix(dst[i], 0, T1, NF), target[...]) + 0.5 * dot(
+            latent[part, :], w_in[2 * D :]
+        )
         return 0
 
-    lax.fori_loop(0, EDGES // T1, base_step, 0)
+    lax.fori_loop(0, EARLY, base_step, 0)
+    all_greeted()
+    halo_moving = exchange(around, lambda s: edge_rows, halo, halo_send, halo_recv)
+    lax.fori_loop(EARLY, EDGES // T1, base_step, 0)
 
     def fill(rows, start):
-        value = dot(rows, w_in[:D])
+        value = 0.5 * dot(rows, w_in[:D])
         table[pl.ds(start, 256)] = value.reshape(256, 4, 128)
 
     for c in range(0, NF, 256):
@@ -277,24 +280,46 @@
     for s in range(0, 8, 2):
         fill(halo[pl.ds(s, 2)].reshape(2 * BND, D), NF + BND * (s + s // 4))
 
-    def pick(first):
-        for e in range(T2):
-            picked[pl.ds(4 * e, 4), :] = table[here["src"][first + e]]
-
-    pick(0)
-
-    def edge_step(i, _):
-        source = jnp.concatenate(
-            [picked[pl.ds(j, T2, stride=4), :] for j in range(4)], axis=1
-        )
-        part = pl.ds(pl.multiple_of(i * T2, T2), T2)
-        hidden = silu(source + latent[part, :].astype(F32)).astype(BF16)
-        pick(jnp.minimum(i + 1, EDGES // T2 - 1) * T2)
-        messages = normed(dot(hidden, here["w_out"][...]), flat_row(here["gain"])).astype(BF16)
-        total[...] += dot(gather_sums(dst[i], NF), messages)
+    quarter = T2 // 4
+
+    def pick(rows, i, t):
+        for e in range(quarter * t, quarter * (t + 1)):
+            rows[pl.ds(4 * e, 4), :] = table[here["src"][i * T2 + e]]
+
+    def edge_sums(messages, i, t):
+        numbers = jnp.concatenate(
+            [dst[i * (T2 // T1) + u] for u in range(T2 // T1)], axis=1
+        ) - NF // 4 * t
+        part = pl.ds(NF // 4 * t, NF // 4)
+        total[part, :] += dot(gather_sums(numbers, NF // 4), messages[...])
+
+    def edge_group(i, rows, messages, next_rows, last_messages):
+        last = jnp.maximum(i - 1, 0)
+        for t in range(4):
+            part = pl.ds(pl.multiple_of(i * T2 + quarter * t, quarter), quarter)
+            half = base[part, :] + jnp.concatenate(
+                [rows[pl.ds(4 * quarter * t + j, quarter, stride=4), :] for j in range(4)],
+                axis=1,
+            )
+            hidden = (half + half * jnp.tanh(half)).astype(BF16)
+            pick(next_rows, jnp.minimum(i + 1, EDGES // T2 - 1), t)
+            messages[pl.ds(quarter * t, quarter), :] = normed(
+                dot(hidden, here["w_out"][...])
+            ).astype(BF16)
+            edge_sums(last_messages, last, t)
+
+    def edge_step(k, _):
+        edge_group(2 * k, picked, messages_a, picked_b, messages_b)
+        edge_group(2 * k + 1, picked_b, messages_b, picked, messages_a)
         return 0
 
-    lax.fori_loop(0, EDGES // T2, edge_step, 0)
+    messages_b[...] = jnp.zeros_like(messages_b)
+    for t in range(4):
+        pick(picked, 0, t)
+    lax.fori_loop(0, EDGES // T2 // 2, edge_step, 0)
+    for t in range(4):
+        edge_sums(messages_b, EDGES // T2 - 1, t)
+    total[...] = total[...] * flat_row(here["gain"])
     fine[...] = node_update(
         nodes[...], total[...].astype(BF16), here["up_in"], here["up_out"], here["up_gain"]
     )
@@ -325,9 +350,9 @@
         w_out=fine_message_out, gain=fine_message_gain,
         up_in=fine_update_in, up_out=fine_update_out, up_gain=fine_update_gain,
         parent1=row(parent_one), weight1=weight_one,
-        src1=row(coarse_src_one), dst1=row(coarse_dst_one),
+        src1=coarse_src_one, dst1=coarse_dst_one,
         parent2=row(parent_two), weight2=weight_two,
-        src2=row(coarse_src_two), dst2=row(coarse_dst_two),
+        src2=coarse_src_two, dst2=coarse_dst_two,
         msg_in=coarse_message_in, msg_out=coarse_message_out, msg_gain=coarse_message_gain,
         cup_in=coarse_update_in, cup_out=coarse_update_out, cup_gain=coarse_update_gain,
     )
@@ -344,8 +369,12 @@
         ]
         + [
             pltpu.VMEM((EDGES, D), BF16),
+            pltpu.VMEM((EDGES, D), F32),
             pltpu.VMEM((NF + 9 * BND, 4, 128), F32),
             pltpu.VMEM((T2 * 4, 128), F32),
+            pltpu.VMEM((T2 * 4, 128), F32),
+            pltpu.VMEM((T2, D), BF16),
+            pltpu.VMEM((T2, D), BF16),
             pltpu.VMEM((NF, D), F32),
             pltpu.VMEM((NF, D), BF16),
             pltpu.VMEM((BND, D), BF16),

time: 99.6 us -> 94.7 us (0.951)
  local copies, waits for them, and re-layouts: 7.36 us -> 2.26 us
    reshape x4 -> x0, local copies, waits for them, and re-layouts: 5.1 us -> none  [row(): return v.reshape(1, -1)]
where the time goes in v3:
time: 94.7 us; the launch traced here: 94.6 us
  Pallas kernels  92.3 us (97%)
  local copies, waits for them, and re-layouts  2.26 us (2%)
    pallas_call x1, Pallas kernels, per_device(): pl.pallas_call(lambda *refs: block_kernel(n_gx, n_gy, *refs), name='block...  92.3 us
    unnamed x1, local copies, waits for them, and re-layouts  2.26 us

profile of v3, /device:TPU:1, one launch (start us, length us, event | category | flops | bytes accessed | tf_op | source)
XLA Modules:
  0.0 94.6 jit_solution(14835536740659936870)
XLA Ops:
  0.0 92.3 %block.1 = bf16[1024,512]{1,0:T(8,128)(2,1)} custom-call(bf16[1024,512]{1,0:T(8,128)(2,1)} %refs_0_.1, s32[1,128]{1,0:T(1,128)} %bitcast.7, bf16[1536,512]{1,0:T(8,128)(2,1)} %refs_2_.1, s32[12,1,512]{2,1,0:T(1,128)} %bitcast.4, s32[6144]{0:T(1024)} %refs_4_.1, bf16[512,512]{1,0:T(8,128)(2,1)} %refs_5_.1, bf16[512]{0:T(512)(128)(2,1)} %refs_6_.1, ...), custom_call_target="tpu_custom_call" | custom-call | tf_op jit(solution)/shard_map/block/pallas_call | solution.py:360
  92.3 2.3 %copy.27 = bf16[1024,512]{1,0:T(8,128)(2,1)} copy(bf16[1024,512]{1,0:T(8,128)(2,1)} %block.1) | data formatting | bytes 2097152

commit v4 on v3

--- a/solution.py
+++ b/solution.py
@@ -18,6 +18,7 @@
 T1 = 512
 T2 = 1024
 EARLY = 4
+PIECES = 2
 OFFSETS = [(k // 3 - 1, k % 3 - 1) for k in range(9) if k != 4]
 
 
@@ -105,15 +106,14 @@
     return jnp.where(down == rows, 1.0, 0.0).astype(BF16)
 
 
-def spread_sums(states, parents, weights, local, rim):
-    numbers = packed_numbers(parents, local, rim)
-    down = lax.broadcasted_iota(jnp.int32, (local + 8 * rim, parents.shape[1]), 0)
+def spread_sums(states, numbers, weights, height):
+    down = lax.broadcasted_iota(jnp.int32, (height, numbers.shape[1]), 0)
     spread = jnp.where(down == numbers, weights, 0.0).astype(BF16)
     return dot(spread, states)
 
 
-def node_update(states, incoming, up_in, up_out, up_gain):
-    update = silu(dot(states, up_in[:D]) + dot(incoming, up_in[D:])).astype(BF16)
+def node_update(states, first, incoming, up_in, up_out, up_gain):
+    update = silu(first + dot(incoming, up_in[D:])).astype(BF16)
     return (
         states.astype(F32) + normed(dot(update, up_out[...]), flat_row(up_gain))
     ).astype(BF16)
@@ -123,24 +123,50 @@
     around, fine, parent1, weight1, src1, dst1, parent2, weight2, src2, dst2,
     msg_in, msg_out, msg_gain, up_in, up_out, up_gain, out,
     sums1, land_a, level1, land_b, sums2, land_c, level2, land_d, new2, land_e, final1, land_f,
-    preact, send_sem, recv_sem,
+    preact, send_sem, recv_sem, piece_send, piece_recv,
 ):
     def swap(i, piece, landing):
         return exchange(around, piece, landing, send_sem.at[i], recv_sem.at[i])
 
     src1, dst1, src2, dst2 = (ref[...].reshape(1, -1) for ref in (src1, dst1, src2, dst2))
     parents = packed_numbers(parent1[...], N1, R1)
-    spread = spread_sums(fine[...], parent1[...], flat_row(weight1), N1, R1)
-    sums1[...] = spread[N1:].astype(BF16)
-    moving = swap(0, lambda s: sums1.at[pl.ds(s * R1, R1)], land_a)
+    weights = flat_row(weight1)
+    sums1[...] = spread_sums(fine[...], parents - N1, weights, 8 * R1).astype(BF16)
+    part = R1 // PIECES
+
+    def piecewise(i, piece, landing):
+        def start(h):
+            copies = [
+                pltpu.make_async_remote_copy(
+                    src_ref=piece(s, h),
+                    dst_ref=landing.at[7 - s, pl.ds(part * h, part)],
+                    send_sem=piece_send.at[i, h, s],
+                    recv_sem=piece_recv.at[i, h, 7 - s],
+                    device_id=who,
+                    device_id_type=MESH,
+                )
+                for s, who in enumerate(around)
+            ]
+            for copy in copies:
+                copy.start()
+            return copies
+
+        return start
+
+    send_sums = piecewise(0, lambda s, h: sums1.at[pl.ds(s * R1 + part * h, part)], land_a)
+    send_rim = piecewise(1, lambda s, h: level1.at[pl.ds(part * h, part)], land_b)
+    arriving = [send_sums(h) for h in range(PIECES)]
+    spread = spread_sums(fine[...], parents, weights, N1)
+    level1[pl.ds(R1, N1 - R1), :] = spread[R1:].astype(BF16)
     down_rows = gather_sums(dst1, N1)
-    finished(moving)
-    rim = spread[:R1]
-    for s in range(8):
-        rim = rim + land_a[s].astype(F32)
-    level1[...] = jnp.concatenate([rim, spread[R1:N1]], axis=0).astype(BF16)
-
-    moving = swap(1, lambda s: level1.at[pl.ds(0, R1)], land_b)
+    moving = []
+    for h in range(PIECES):
+        finished(arriving[h])
+        rim = spread[part * h : part * (h + 1)]
+        for s in range(8):
+            rim = rim + land_a[s, pl.ds(part * h, part)].astype(F32)
+        level1[pl.ds(part * h, part), :] = rim.astype(BF16)
+        moving = moving + send_rim(h)
     own = dot(level1[...], msg_in[:D]).astype(BF16)
     mine = dot(level1[...], msg_in[D:]).astype(BF16)
     numbers = packed_numbers(src1, N1, R1)
@@ -148,6 +174,7 @@
         preact[pl.ds(t, 512), :] = dot(pick_matrix(numbers, t, 512, N1), own) + dot(
             pick_matrix(dst1, t, 512, N1), mine
         )
+    first = dot(level1[...], up_in[:D])
     finished(moving)
     beyond = dot(land_b[...].reshape(8 * R1, D), msg_in[:D]).astype(BF16)
     incoming = jnp.zeros((N1, D), F32)
@@ -157,11 +184,13 @@
         ).astype(BF16)
         messages = normed(dot(hidden, msg_out[...]), flat_row(msg_gain)).astype(BF16)
         incoming = incoming + dot(down_rows[:, t : t + 512], messages)
-    new1 = node_update(level1[...], incoming.astype(BF16), up_in, up_out, up_gain)
-
-    spread = spread_sums(new1, parent2[...], flat_row(weight2), N2, R2)
-    sums2[...] = spread[N2:].astype(BF16)
+    new1 = node_update(level1[...], first, incoming.astype(BF16), up_in, up_out, up_gain)
+
+    parents2 = packed_numbers(parent2[...], N2, R2)
+    weights = flat_row(weight2)
+    sums2[...] = spread_sums(new1, parents2 - N2, weights, 8 * R2).astype(BF16)
     moving = swap(2, lambda s: sums2.at[pl.ds(s * R2, R2)], land_c)
+    spread = spread_sums(new1, parents2, weights, N2)
     finished(moving)
     rim = spread[:R2]
     for s in range(8):
@@ -176,12 +205,13 @@
     start = dot(pick_matrix(dst2, 0, E2, 128), jnp.concatenate([mine, pad], axis=0)) + dot(
         pick_matrix(numbers, 0, E2, 128), jnp.concatenate([own, pad], axis=0)
     )
+    first = dot(level2[...], up_in[:D])
     finished(moving)
     beyond = dot(land_d[...].reshape(8 * R2, D), msg_in[:D]).astype(BF16)
     hidden = silu(start + dot(pick_matrix(numbers, 0, E2, 8 * R2, N2), beyond)).astype(BF16)
     messages = normed(dot(hidden, msg_out[...]), flat_row(msg_gain)).astype(BF16)
     incoming = dot(gather_sums(dst2, N2), messages).astype(BF16)
-    new2[...] = node_update(level2[...], incoming, up_in, up_out, up_gain)
+    new2[...] = node_update(level2[...], first, incoming, up_in, up_out, up_gain)
 
     moving = swap(4, lambda s: new2.at[pl.ds(0, R2)], land_e)
     numbers = packed_numbers(parent2[...], N2, R2)
@@ -223,10 +253,10 @@
     latent_far, out = refs[count], refs[count + 1]
     here = dict(zip(LOADS, refs[count + 2 : 2 * count + 2]))
     (
-        latent, base, table, picked, picked_b, messages_a, messages_b, total, target, edge_rows, halo,
+        latent, base, first, table, picked, messages_a, messages_b, total, target, edge_rows, halo,
         fine, sums1, land_a, level1, land_b, sums2, land_c, level2, land_d, new2, land_e,
         final1, land_f, preact, load_sem, latent_sem, halo_send, halo_recv,
-        send_sem, recv_sem,
+        send_sem, recv_sem, piece_send, piece_recv,
     ) = refs[2 * count + 2 :]
     around = neighbours(n_gx, n_gy)
     greet(around)
@@ -276,6 +306,7 @@
     total[...] = jnp.zeros_like(total)
     for name in LOADS[5:]:
         loads[name].wait()
+    first[...] = dot(nodes[...], here["up_in"][:D])
     finished(halo_moving)
     for s in range(0, 8, 2):
         fill(halo[pl.ds(s, 2)].reshape(2 * BND, D), NF + BND * (s + s // 4))
@@ -283,8 +314,8 @@
     quarter = T2 // 4
 
     def pick(rows, i, t):
-        for e in range(quarter * t, quarter * (t + 1)):
-            rows[pl.ds(4 * e, 4), :] = table[here["src"][i * T2 + e]]
+        for e in range(quarter):
+            rows[pl.ds(4 * e, 4), :] = table[here["src"][i * T2 + quarter * t + e]]
 
     def edge_sums(messages, i, t):
         numbers = jnp.concatenate(
@@ -293,41 +324,41 @@
         part = pl.ds(NF // 4 * t, NF // 4)
         total[part, :] += dot(gather_sums(numbers, NF // 4), messages[...])
 
-    def edge_group(i, rows, messages, next_rows, last_messages):
+    def edge_group(i, messages, last_messages):
         last = jnp.maximum(i - 1, 0)
+        following = jnp.minimum(i + 1, EDGES // T2 - 1)
         for t in range(4):
             part = pl.ds(pl.multiple_of(i * T2 + quarter * t, quarter), quarter)
             half = base[part, :] + jnp.concatenate(
-                [rows[pl.ds(4 * quarter * t + j, quarter, stride=4), :] for j in range(4)],
+                [picked[t % 2, pl.ds(j, quarter, stride=4), :] for j in range(4)],
                 axis=1,
             )
             hidden = (half + half * jnp.tanh(half)).astype(BF16)
-            pick(next_rows, jnp.minimum(i + 1, EDGES // T2 - 1), t)
+            pick(picked.at[(t + 1) % 2], i if t < 3 else following, (t + 1) % 4)
             messages[pl.ds(quarter * t, quarter), :] = normed(
                 dot(hidden, here["w_out"][...])
             ).astype(BF16)
             edge_sums(last_messages, last, t)
 
     def edge_step(k, _):
-        edge_group(2 * k, picked, messages_a, picked_b, messages_b)
-        edge_group(2 * k + 1, picked_b, messages_b, picked, messages_a)
+        edge_group(2 * k, messages_a, messages_b)
+        edge_group(2 * k + 1, messages_b, messages_a)
         return 0
 
     messages_b[...] = jnp.zeros_like(messages_b)
-    for t in range(4):
-        pick(picked, 0, t)
+    pick(picked.at[0], 0, 0)
     lax.fori_loop(0, EDGES // T2 // 2, edge_step, 0)
     for t in range(4):
         edge_sums(messages_b, EDGES // T2 - 1, t)
     total[...] = total[...] * flat_row(here["gain"])
     fine[...] = node_update(
-        nodes[...], total[...].astype(BF16), here["up_in"], here["up_out"], here["up_gain"]
+        nodes[...], first[...], total[...].astype(BF16), here["up_in"], here["up_out"], here["up_gain"]
     )
 
     coarse_part(
         around, fine, *[here[name] for name in LOADS[10:]], out,
         sums1, land_a, level1, land_b, sums2, land_c, level2, land_d, new2, land_e,
-        final1, land_f, preact, send_sem, recv_sem,
+        final1, land_f, preact, send_sem, recv_sem, piece_send, piece_recv,
     )
 
 
@@ -370,9 +401,9 @@
         + [
             pltpu.VMEM((EDGES, D), BF16),
             pltpu.VMEM((EDGES, D), F32),
+            pltpu.VMEM((NF, D), F32),
             pltpu.VMEM((NF + 9 * BND, 4, 128), F32),
-            pltpu.VMEM((T2 * 4, 128), F32),
-            pltpu.VMEM((T2 * 4, 128), F32),
+            pltpu.VMEM((2, T2, 128), F32),
             pltpu.VMEM((T2, D), BF16),
             pltpu.VMEM((T2, D), BF16),
             pltpu.VMEM((NF, D), F32),
@@ -399,6 +430,8 @@
             pltpu.SemaphoreType.DMA((8,)),
             pltpu.SemaphoreType.DMA((6, 8)),
             pltpu.SemaphoreType.DMA((6, 8)),
+            pltpu.SemaphoreType.DMA((2, PIECES, 8)),
+            pltpu.SemaphoreType.DMA((2, PIECES, 8)),
         ],
         compiler_params=pltpu.CompilerParams(
             collective_id=0, has_side_effects=True, vmem_limit_bytes=58 * 2**20

time: 94.7 us -> 94.3 us (level)
  no operation moved by 1% of the time
where the time goes in v4:
time: 94.3 us; the launch traced here: 94.2 us
  Pallas kernels  91.9 us (97%)
  local copies, waits for them, and re-layouts  2.26 us (2%)
    pallas_call x1, Pallas kernels, per_device(): pl.pallas_call(lambda *refs: block_kernel(n_gx, n_gy, *refs), name='block...  91.9 us
    unnamed x1, local copies, waits for them, and re-layouts  2.26 us

profile of v4, /device:TPU:1, one launch (start us, length us, event | category | flops | bytes accessed | tf_op | source)
XLA Modules:
  0.0 94.2 jit_solution(2748247488976732204)
XLA Ops:
  0.0 91.9 %block.1 = bf16[1024,512]{1,0:T(8,128)(2,1)} custom-call(bf16[1024,512]{1,0:T(8,128)(2,1)} %refs_0_.1, s32[1,128]{1,0:T(1,128)} %bitcast.7, bf16[1536,512]{1,0:T(8,128)(2,1)} %refs_2_.1, s32[12,1,512]{2,1,0:T(1,128)} %bitcast.4, s32[6144]{0:T(1024)} %refs_4_.1, bf16[512,512]{1,0:T(8,128)(2,1)} %refs_5_.1, bf16[512]{0:T(512)(128)(2,1)} %refs_6_.1, ...), custom_call_target="tpu_custom_call" | custom-call | tf_op jit(solution)/shard_map/block/pallas_call | solution.py:391
  91.9 2.3 %copy.27 = bf16[1024,512]{1,0:T(8,128)(2,1)} copy(bf16[1024,512]{1,0:T(8,128)(2,1)} %block.1) | data formatting | bytes 2097152

commit v5 on v4

--- a/solution.py
+++ b/solution.py
@@ -134,7 +134,7 @@
     sums1[...] = spread_sums(fine[...], parents - N1, weights, 8 * R1).astype(BF16)
     part = R1 // PIECES
 
-    def piecewise(i, piece, landing):
+    def piecewise(i, part, piece, landing):
         def start(h):
             copies = [
                 pltpu.make_async_remote_copy(
@@ -153,8 +153,8 @@
 
         return start
 
-    send_sums = piecewise(0, lambda s, h: sums1.at[pl.ds(s * R1 + part * h, part)], land_a)
-    send_rim = piecewise(1, lambda s, h: level1.at[pl.ds(part * h, part)], land_b)
+    send_sums = piecewise(0, part, lambda s, h: sums1.at[pl.ds(s * R1 + part * h, part)], land_a)
+    send_rim = piecewise(1, part, lambda s, h: level1.at[pl.ds(part * h, part)], land_b)
     arriving = [send_sums(h) for h in range(PIECES)]
     spread = spread_sums(fine[...], parents, weights, N1)
     level1[pl.ds(R1, N1 - R1), :] = spread[R1:].astype(BF16)
@@ -189,15 +189,20 @@
     parents2 = packed_numbers(parent2[...], N2, R2)
     weights = flat_row(weight2)
     sums2[...] = spread_sums(new1, parents2 - N2, weights, 8 * R2).astype(BF16)
-    moving = swap(2, lambda s: sums2.at[pl.ds(s * R2, R2)], land_c)
+    small = R2 // PIECES
+    send_sums = piecewise(2, small, lambda s, h: sums2.at[pl.ds(s * R2 + small * h, small)], land_c)
+    send_rim = piecewise(3, small, lambda s, h: level2.at[pl.ds(small * h, small)], land_d)
+    arriving = [send_sums(h) for h in range(PIECES)]
     spread = spread_sums(new1, parents2, weights, N2)
-    finished(moving)
-    rim = spread[:R2]
-    for s in range(8):
-        rim = rim + land_c[s].astype(F32)
-    level2[...] = jnp.concatenate([rim, spread[R2:N2]], axis=0).astype(BF16)
-
-    moving = swap(3, lambda s: level2.at[pl.ds(0, R2)], land_d)
+    level2[pl.ds(R2, N2 - R2), :] = spread[R2:].astype(BF16)
+    moving = []
+    for h in range(PIECES):
+        finished(arriving[h])
+        rim = spread[small * h : small * (h + 1)]
+        for s in range(8):
+            rim = rim + land_c[s, pl.ds(small * h, small)].astype(F32)
+        level2[pl.ds(small * h, small), :] = rim.astype(BF16)
+        moving = moving + send_rim(h)
     mine = dot(level2[...], msg_in[D:]).astype(BF16)
     own = dot(level2[...], msg_in[:D]).astype(BF16)
     numbers = packed_numbers(src2, N2, R2)
@@ -253,7 +258,7 @@
     latent_far, out = refs[count], refs[count + 1]
     here = dict(zip(LOADS, refs[count + 2 : 2 * count + 2]))
     (
-        latent, base, first, table, picked, messages_a, messages_b, total, target, edge_rows, halo,
+        latent, base, first, table, picked, picked_b, messages_a, messages_b, total, target, edge_rows, halo,
         fine, sums1, land_a, level1, land_b, sums2, land_c, level2, land_d, new2, land_e,
         final1, land_f, preact, load_sem, latent_sem, halo_send, halo_recv,
         send_sem, recv_sem, piece_send, piece_recv,
@@ -314,8 +319,8 @@
     quarter = T2 // 4
 
     def pick(rows, i, t):
-        for e in range(quarter):
-            rows[pl.ds(4 * e, 4), :] = table[here["src"][i * T2 + quarter * t + e]]
+        for e in range(quarter * t, quarter * (t + 1)):
+            rows[pl.ds(4 * e, 4), :] = table[here["src"][i * T2 + e]]
 
     def edge_sums(messages, i, t):
         numbers = jnp.concatenate(
@@ -324,29 +329,30 @@
         part = pl.ds(NF // 4 * t, NF // 4)
         total[part, :] += dot(gather_sums(numbers, NF // 4), messages[...])
 
-    def edge_group(i, messages, last_messages):
+    def edge_group(i, rows, messages, next_rows, last_messages):
         last = jnp.maximum(i - 1, 0)
         following = jnp.minimum(i + 1, EDGES // T2 - 1)
         for t in range(4):
             part = pl.ds(pl.multiple_of(i * T2 + quarter * t, quarter), quarter)
             half = base[part, :] + jnp.concatenate(
-                [picked[t % 2, pl.ds(j, quarter, stride=4), :] for j in range(4)],
+                [rows[pl.ds(4 * quarter * t + j, quarter, stride=4), :] for j in range(4)],
                 axis=1,
             )
             hidden = (half + half * jnp.tanh(half)).astype(BF16)
-            pick(picked.at[(t + 1) % 2], i if t < 3 else following, (t + 1) % 4)
+            pick(next_rows, following, t)
             messages[pl.ds(quarter * t, quarter), :] = normed(
                 dot(hidden, here["w_out"][...])
             ).astype(BF16)
             edge_sums(last_messages, last, t)
 
     def edge_step(k, _):
-        edge_group(2 * k, messages_a, messages_b)
-        edge_group(2 * k + 1, messages_b, messages_a)
+        edge_group(2 * k, picked, messages_a, picked_b, messages_b)
+        edge_group(2 * k + 1, picked_b, messages_b, picked, messages_a)
         return 0
 
     messages_b[...] = jnp.zeros_like(messages_b)
-    pick(picked.at[0], 0, 0)
+    for t in range(4):
+        pick(picked, 0, t)
     lax.fori_loop(0, EDGES // T2 // 2, edge_step, 0)
     for t in range(4):
         edge_sums(messages_b, EDGES // T2 - 1, t)
@@ -403,7 +409,8 @@
             pltpu.VMEM((EDGES, D), F32),
             pltpu.VMEM((NF, D), F32),
             pltpu.VMEM((NF + 9 * BND, 4, 128), F32),
-            pltpu.VMEM((2, T2, 128), F32),
+            pltpu.VMEM((T2 * 4, 128), F32),
+            pltpu.VMEM((T2 * 4, 128), F32),
             pltpu.VMEM((T2, D), BF16),
             pltpu.VMEM((T2, D), BF16),
             pltpu.VMEM((NF, D), F32),
@@ -430,8 +437,8 @@
             pltpu.SemaphoreType.DMA((8,)),
             pltpu.SemaphoreType.DMA((6, 8)),
             pltpu.SemaphoreType.DMA((6, 8)),
-            pltpu.SemaphoreType.DMA((2, PIECES, 8)),
-            pltpu.SemaphoreType.DMA((2, PIECES, 8)),
+            pltpu.SemaphoreType.DMA((4, PIECES, 8)),
+            pltpu.SemaphoreType.DMA((4, PIECES, 8)),
         ],
         compiler_params=pltpu.CompilerParams(
             collective_id=0, has_side_effects=True, vmem_limit_bytes=58 * 2**20

time: 94.3 us -> 94.2 us (level)
  no operation moved by 1% of the time
where the time goes in v5:
time: 94.2 us; the launch traced here: 94.1 us
  Pallas kernels  91.8 us (97%)
  local copies, waits for them, and re-layouts  2.26 us (2%)
    pallas_call x1, Pallas kernels, per_device(): pl.pallas_call(lambda *refs: block_kernel(n_gx, n_gy, *refs), name='block...  91.8 us
    unnamed x1, local copies, waits for them, and re-layouts  2.26 us

profile of v5, /device:TPU:1, one launch (start us, length us, event | category | flops | bytes accessed | tf_op | source)
XLA Modules:
  0.0 94.1 jit_solution(9435661412273487819)
XLA Ops:
  0.0 91.8 %block.1 = bf16[1024,512]{1,0:T(8,128)(2,1)} custom-call(bf16[1024,512]{1,0:T(8,128)(2,1)} %refs_0_.1, s32[1,128]{1,0:T(1,128)} %bitcast.7, bf16[1536,512]{1,0:T(8,128)(2,1)} %refs_2_.1, s32[12,1,512]{2,1,0:T(1,128)} %bitcast.4, s32[6144]{0:T(1024)} %refs_4_.1, bf16[512,512]{1,0:T(8,128)(2,1)} %refs_5_.1, bf16[512]{0:T(512)(128)(2,1)} %refs_6_.1, ...), custom_call_target="tpu_custom_call" | custom-call | tf_op jit(solution)/shard_map/block/pallas_call | solution.py:397
  91.8 2.3 %copy.27 = bf16[1024,512]{1,0:T(8,128)(2,1)} copy(bf16[1024,512]{1,0:T(8,128)(2,1)} %block.1) | data formatting | bytes 2097152
